TPU v7x, 32 devices: a whole 2x2x4 slice. The times are simulated.
32 devices in a mesh: dp: 8 (over z, y), rep: 4 (over x, core).
Axes of the slice: x: 2, y: 2, z: 4, core: 2. Of those that a mesh axis runs over, the one named last changes fastest.
Arguments:
- grads: bfloat16 [32, 4096, 512], P(('dp', 'rep')), may hold values from -1000 to 1000
- master: float32 [4096, 512], P('dp'), may hold values from -3 to 3
- first_moment: float32 [4096, 512], P('dp'), may hold values from -2 to 2
- second_moment: float32 [4096, 512], P('dp'), may hold values from 0.01 to 1
Outputs:
- weights: bfloat16 [4096, 512], replicated
- new_master: float32 [4096, 512], P('dp')
- new_first: float32 [4096, 512], P('dp')
- new_second: float32 [4096, 512], P('dp')
All inputs are finite; a program needn't handle non-finite values.
Results may differ from a plain program's by a relative error of at most 0.001.
Values may be sent and summed in bfloat16 or wider, within the bound.
A program may use at most 64 MiB of HBM per device.

v0:
```python
import functools
import math

import jax
import jax.numpy as jnp
from jax import lax
from jax.experimental import pallas as pl
from jax.experimental.pallas import tpu as pltpu
from jax.sharding import PartitionSpec as P

STEP = 20
MESH = pl.DeviceIdType.MESH
F32 = jnp.float32
PIECES, TRAIL = 2, (2, 4)
W_PIECES, W_TRAIL = 2, (2, 3)
VMEM_BYTES = 63 * 1024 * 1024


def adam_update(clipped, master, first_moment, second_moment):
    new_first = 0.9 * first_moment + 0.1 * clipped
    new_second = 0.95 * second_moment + 0.05 * clipped * clipped
    first_hat = new_first / (1.0 - 0.9**STEP)
    second_hat = new_second / (1.0 - 0.95**STEP)
    update = first_hat / (jnp.sqrt(second_hat) + 1e-08)
    new_master = master - 0.01 * (update + 0.1 * master)
    return (new_master, new_first, new_second)


def clip_factor(squares, entries):
    threshold = 4.0 * math.sqrt(entries)
    return jnp.minimum(1.0, threshold / (jnp.sqrt(squares) + 1e-06))


def kernel(
    Z, R, entries,
    g, m_in, f_in, s_in,
    W, M, F, Q,
    mine, swapped, S, RA, RB, R2, R3, V, N,
    load_sem, state_sem,
    g_sem, a1_sem, b1_sem, a2_sem, b2_sem, z_sem, n_sem, v_sem,
    gz_sem, ga_sem, gb_sem, ha_sem, hb_sem, gc_sem,
):
    D = 2 * Z
    n = D * R
    d, r = lax.axis_index("dp"), lax.axis_index("rep")
    z, y = d // 2, d % 2
    x, c = r // 2, r % 2
    me = d * R + r
    C, G = PIECES * Z, W_PIECES * Z
    to_x = (d, (1 - x) * 2 + c)
    to_y = (z * 2 + 1 - y, r)
    to_c = (d, x * 2 + 1 - c)

    def to_z(other):
        return (other * 2 + y, r)

    def push(src, dst, sems, index, device):
        return pltpu.make_async_remote_copy(
            src_ref=src, dst_ref=dst, send_sem=sems.at[(0,) + index], recv_sem=sems.at[(1,) + index],
            device_id=device, device_id_type=MESH,
        )

    def dest(k):
        return (z + 1 + k) % Z

    def cols(q):
        width = g.shape[-1] // PIECES
        return pl.ds(pl.multiple_of((q % PIECES) * width, width), width)

    def w_cols(q):
        width = g.shape[-1] // W_PIECES
        return pl.ds(pl.multiple_of((q % W_PIECES) * width, width), width)

    barrier = pltpu.get_barrier_semaphore()

    @pl.loop(1, n)
    def _(k):
        t = (me + k) % n
        pl.semaphore_signal(barrier, inc=1, device_id=(t // R, t % R), device_id_type=MESH)

    def load(k):
        return pltpu.make_async_copy(
            g.at[dest(k // PIECES), :, c, :, :, :, cols(k)], mine.at[k // PIECES, :, :, :, :, cols(k)], load_sem.at[k]
        )

    @pl.loop(0, C)
    def _(k):
        load(k).start()

    states = [
        pltpu.make_async_copy(a, b, state_sem.at[i])
        for i, (a, b) in enumerate([(m_in, M), (f_in, F), (s_in, Q)])
    ]
    for copy in states:
        copy.start()
    pl.semaphore_wait(barrier, n - 1)

    def swap(k):
        return push(
            g.at[dest(k // PIECES), :, 1 - c, :, :, :, cols(k)], swapped.at[k // PIECES, :, :, :, :, cols(k)],
            g_sem, (k,), to_c,
        )

    @pl.loop(0, C)
    def _(k):
        swap(k).start()

    def first_a(k):
        i, p = k // PIECES, cols(k)
        return push(S.at[i, :, 1 - x, 0, :, p], RA.at[i, :, :, p], a1_sem, (k,), to_x)

    def first_b(k):
        i, p = k // PIECES, cols(k)
        return push(S.at[i, 1 - y, :, 1, :, p], RB.at[i, :, :, p], b1_sem, (k,), to_y)

    def second_a(k):
        i, p = k // PIECES, cols(k)
        return push(S.at[i, 1 - y, x, 0, :, p], R2.at[i, 0, :, p], a2_sem, (k,), to_y)

    def second_b(k):
        i, p = k // PIECES, cols(k)
        return push(S.at[i, y, 1 - x, 1, :, p], R2.at[i, 1, :, p], b2_sem, (k,), to_x)

    def along_z(k):
        i, p = k // PIECES, cols(k)
        return push(S.at[i, y, x, :, :, p], R3.at[i, :, :, p], z_sem, (k,), to_z(dest(i)))

    @pl.loop(0, C + TRAIL[1])
    def _(step):
        @pl.when(step < C)
        def _():
            k = step
            i, p = k // PIECES, cols(k)
            load(k).wait()
            swap(k).wait_recv()
            S[i, :, :, :, :, p] = mine[i, :, :, :, :, p].astype(F32) + swapped[i, :, :, :, :, p].astype(F32)
            first_a(k).start()
            first_b(k).start()

        @pl.when((step >= TRAIL[0]) & (step < C + TRAIL[0]))
        def _():
            k = step - TRAIL[0]
            i, p = k // PIECES, cols(k)
            first_a(k).wait_recv()
            S[i, :, x, 0, :, p] = S[i, :, x, 0, :, p] + RA[i, :, :, p]
            second_a(k).start()
            first_b(k).wait_recv()
            S[i, y, :, 1, :, p] = S[i, y, :, 1, :, p] + RB[i, :, :, p]
            second_b(k).start()

        @pl.when(step >= TRAIL[1])
        def _():
            k = step - TRAIL[1]
            i, p = k // PIECES, cols(k)
            second_a(k).wait_recv()
            second_b(k).wait_recv()
            S[i, y, x, :, :, p] = S[i, y, x, :, :, p] + R2[i, :, :, p]

            @pl.when(k < C - PIECES)
            def _():
                along_z(k).start()

    @pl.loop(0, C - PIECES)
    def _(k):
        i, p = k // PIECES, cols(k)
        along_z(k).wait_recv()
        S[Z - 1, y, x, :, :, p] = S[Z - 1, y, x, :, :, p] + R3[i, :, :, p]

    total = S[Z - 1, y, x]
    V[c, x] = total
    lanes = jnp.sum((total * total).reshape(-1, total.shape[-1]), axis=0, keepdims=True)
    N[me] = sum(lanes[:, i : i + 128] for i in range(0, total.shape[-1], 128))

    def norm_part(k):
        t = (me + k) % n
        return push(N.at[me], N.at[me], n_sem, (k,), (t // R, t % R))

    def norm_recv(k):
        t = (me + n - k) % n
        return push(N.at[t], N.at[t], n_sem, (k,), (t // R, t % R))

    @pl.loop(1, n)
    def _(k):
        norm_part(k).start()

    v_x = push(V.at[c, x], V.at[c, x], v_sem, (0,), to_x)
    v_c = push(V.at[c, x], V.at[c, x], v_sem, (1,), to_c)
    v_xc = push(V.at[c, 1 - x], V.at[c, 1 - x], v_sem, (2,), to_c)
    got_x = push(V.at[c, 1 - x], V.at[c, 1 - x], v_sem, (0,), to_x)
    got_c = push(V.at[1 - c, x], V.at[1 - c, x], v_sem, (1,), to_c)
    got_xc = push(V.at[1 - c, 1 - x], V.at[1 - c, 1 - x], v_sem, (2,), to_c)
    v_x.start()
    v_c.start()

    for copy in states:
        copy.wait()

    @pl.loop(1, n)
    def _(k):
        norm_recv(k).wait_recv()

    factor = clip_factor(jnp.sum(N[...]), entries)

    def update(cc, xx):
        new_master, new_first, new_second = adam_update(factor * V[cc, xx], M[cc, xx], F[cc, xx], Q[cc, xx])
        M[cc, xx] = new_master
        F[cc, xx] = new_first
        Q[cc, xx] = new_second
        return new_master

    W[z, y, c, x] = update(c, x).astype(jnp.bfloat16)

    def source(b):
        return (z + Z - b // W_PIECES) % Z

    def gather_z(j):
        block = W.at[z, y, c, x, :, :, w_cols(j)]
        return push(block, block, gz_sem, (j,), to_z(dest(j // W_PIECES)))

    def got_z(j):
        block = W.at[source(j + W_PIECES), y, c, x, :, :, w_cols(j)]
        return push(block, block, gz_sem, (j,), to_z(dest(j // W_PIECES)))

    @pl.loop(0, G - W_PIECES)
    def _(j):
        gather_z(j).start()

    def same(ref, sems, b, device):
        return push(ref, ref, sems, (b,), device)

    def ga(b, yy):
        return same(W.at[source(b), yy, c, x, 0, :, w_cols(b)], ga_sem, b, to_y)

    def gb(b, xx):
        return same(W.at[source(b), y, c, xx, 1, :, w_cols(b)], gb_sem, b, to_x)

    def ha(b, xx):
        return same(W.at[source(b), :, c, xx, 0, :, w_cols(b)], ha_sem, b, to_x)

    def hb(b, yy):
        return same(W.at[source(b), yy, c, :, 1, :, w_cols(b)], hb_sem, b, to_y)

    def gc(b, cc):
        return same(W.at[source(b), :, cc, :, :, :, w_cols(b)], gc_sem, b, to_c)

    @pl.loop(0, G + W_TRAIL[1])
    def _(step):
        @pl.when((step >= W_TRAIL[0]) & (step < G + W_TRAIL[0]))
        def _():
            b = step - W_TRAIL[0]
            ga(b, 1 - y).wait_recv()
            ha(b, x).start()
            gb(b, 1 - x).wait_recv()
            hb(b, y).start()

        @pl.when(step < G)
        def _():
            b = step

            @pl.when(b >= W_PIECES)
            def _():
                got_z(b - W_PIECES).wait_recv()

            ga(b, y).start()
            gb(b, x).start()

        @pl.when(step == 1)
        def _():
            got_x.wait_recv()
            v_xc.start()
            update(c, 1 - x)

        @pl.when(step == 2)
        def _():
            got_c.wait_recv()
            update(1 - c, x)

        @pl.when(step == 3)
        def _():
            got_xc.wait_recv()
            update(1 - c, 1 - x)

        @pl.when(step >= W_TRAIL[1])
        def _():
            b = step - W_TRAIL[1]
            ha(b, 1 - x).wait_recv()
            hb(b, 1 - y).wait_recv()
            gc(b, c).start()

    @pl.loop(0, G)
    def _(b):
        gc(b, 1 - c).wait_recv()

    v_x.wait_send()
    v_c.wait_send()
    v_xc.wait_send()

    @pl.loop(1, n)
    def _(k):
        norm_part(k).wait_send()

    @pl.loop(0, C)
    def _(k):
        swap(k).wait_send()
        first_a(k).wait_send()
        first_b(k).wait_send()
        second_a(k).wait_send()
        second_b(k).wait_send()

    @pl.loop(0, C - PIECES)
    def _(k):
        along_z(k).wait_send()

    @pl.loop(0, G)
    def _(b):
        ga(b, y).wait_send()
        gb(b, x).wait_send()
        ha(b, x).wait_send()
        hb(b, y).wait_send()
        gc(b, c).wait_send()

    @pl.loop(0, G - W_PIECES)
    def _(j):
        gather_z(j).wait_send()


def write_out(*refs):
    srcs, dsts, sems = refs[:4], refs[4:8], refs[8]
    copies = [pltpu.make_async_copy(a, b, sems.at[i]) for i, (a, b) in enumerate(zip(srcs, dsts))]
    for copy in copies:
        copy.start()
    for copy in copies:
        copy.wait()


def body(D, R, grads, master, first_moment, second_moment):
    rows, cols = grads.shape[1:]
    Z, n = D // 2, D * R
    t = rows // (D * R * 2)
    hbm = pl.BlockSpec(memory_space=pltpu.HBM)
    vmem = pl.BlockSpec(memory_space=pltpu.VMEM)
    bf16 = jnp.bfloat16
    part = (2, 2, 2, t, cols)
    dma = pltpu.SemaphoreType.DMA
    shapes = [((Z, 2) + part, bf16)] + [(part, F32)] * 3
    held_bytes = sum(math.prod(dims) * jnp.dtype(kind).itemsize for dims, kind in shapes)
    held = pl.pallas_call(
        functools.partial(kernel, Z, R, rows * cols),
        out_shape=[pltpu.VMEM(*shape) for shape in shapes],
        in_specs=[hbm] * 4,
        out_specs=[vmem] * 4,
        scratch_shapes=[
            pltpu.VMEM((Z,) + part, bf16),
            pltpu.VMEM((Z,) + part, bf16),
            pltpu.VMEM((Z,) + part, F32),
            pltpu.VMEM((Z, 2, t, cols), F32),
            pltpu.VMEM((Z, 2, t, cols), F32),
            pltpu.VMEM((Z, 2, t, cols), F32),
            pltpu.VMEM((Z - 1, 2, t, cols), F32),
            pltpu.VMEM(part, F32),
            pltpu.VMEM((n, 1, 128), F32),
            dma((PIECES * Z,)), dma((3,)),
            dma((2, PIECES * Z)), dma((2, PIECES * Z)), dma((2, PIECES * Z)),
            dma((2, PIECES * Z)), dma((2, PIECES * Z)), dma((2, PIECES * Z)),
            dma((2, n)), dma((2, 3)),
            dma((2, W_PIECES * Z)), dma((2, W_PIECES * Z)), dma((2, W_PIECES * Z)),
            dma((2, W_PIECES * Z)), dma((2, W_PIECES * Z)), dma((2, W_PIECES * Z)),
        ],
        compiler_params=pltpu.CompilerParams(
            collective_id=0, has_side_effects=True, vmem_limit_bytes=VMEM_BYTES - held_bytes
        ),
    )(
        grads.reshape((Z, 2) + part),
        master.reshape(part), first_moment.reshape(part), second_moment.reshape(part),
    )
    outs = pl.pallas_call(
        write_out,
        out_shape=[jax.ShapeDtypeStruct(*shape) for shape in shapes],
        in_specs=[vmem] * 4,
        out_specs=[hbm] * 4,
        scratch_shapes=[dma((4,))],
        compiler_params=pltpu.CompilerParams(vmem_limit_bytes=1024 * 1024),
    )(*held)
    weights, new_master, new_first, new_second = outs
    block = (rows // D, cols)
    return (weights.reshape(rows, cols), new_master.reshape(block), new_first.reshape(block), new_second.reshape(block))


def solution(mesh):
    D, R = mesh.shape["dp"], mesh.shape["rep"]
    assert R == 4 and D % 2 == 0
    in_specs = (P(("dp", "rep"), None, None), P("dp", None), P("dp", None), P("dp", None))
    out_specs = (P(), P("dp", None), P("dp", None), P("dp", None))
    return jax.shard_map(
        functools.partial(body, D, R), mesh=mesh, in_specs=in_specs, out_specs=out_specs, check_vma=False
    )
```

profile of v0, /device:TPU:1, one launch (start us, length us, event | category | flops | bytes accessed | tf_op | source)
XLA Modules:
  0.0 83.2 jit_solution(16163337585214474773)
XLA Ops:
  0.6 79.6 %shard_map.75 = (bf16[4,2,2,2,2,64,512]{6,5,4,3,2,1,0:T(8,128)(2,1)S(1)}, f32[2,2,2,64,512]{4,3,2,1,0:T(8,128)S(1)}, f32[2,2,2,64,512]{4,3,2,1,0:T(8,128)S(1)}, f32[2,2,2,64,512]{4,3,2,1,0:T(8,128)S(1)}) custom-call(bf16[4,2,2,2,2,64,512]{6,5,4,3,2,1,0:T(8,128)(2,1)} %bitcast.8, f32[2,2,2,64,512]{4,3,2,1,0:T(8,128)} %bitcast.9, ...), custom_call_target="tpu_custom_call" | custom-call | tf_op jit(solution)/shard_map/pallas_call | solution.py:347
  80.2 3.0 %shard_map.76 = (bf16[4,2,2,2,2,64,512]{6,5,4,3,2,1,0:T(8,128)(2,1)}, f32[2,2,2,64,512]{4,3,2,1,0:T(8,128)}, f32[2,2,2,64,512]{4,3,2,1,0:T(8,128)}, f32[2,2,2,64,512]{4,3,2,1,0:T(8,128)}) custom-call(bf16[4,2,2,2,2,64,512]{6,5,4,3,2,1,0:T(8,128)(2,1)S(1)} %get-tuple-element.12.refs_0_, f32[2,2,2,64,512]{4,3,2,1,0:T(8,128)S(1)} %get-tuple-element.13.refs_1_, ...), custom_call_target="tpu_custom_call" | custom-call | tf_op jit(solution)/shard_map/pallas_call | solution.py:376
where the time goes:
time: 83.5 us; the launch traced here: 83.2 us
  Pallas kernels  82.6 us (99%)
    pallas_call x1, Pallas kernels, body(): pl.pallas_call(functools.partial(kernel, Z, R, rows * cols), out_shape=[p...  79.6 us
    pallas_call x1, Pallas kernels, body(): pl.pallas_call(write_out, out_shape=[jax.ShapeDtypeStruct(*shape) for sha...  3.02 us

commit v1 on v0

--- a/solution.py
+++ b/solution.py
@@ -14,6 +14,7 @@
 PIECES, TRAIL = 2, (2, 4)
 W_PIECES, W_TRAIL = 2, (2, 3)
 VMEM_BYTES = 63 * 1024 * 1024
+TOP = 2.0**14
 
 
 def adam_update(clipped, master, first_moment, second_moment):
@@ -31,13 +32,26 @@
     return jnp.minimum(1.0, threshold / (jnp.sqrt(squares) + 1e-06))
 
 
+def encode(value, scale):
+    u = value * scale
+    u2 = u * u
+    u4 = u2 * u2
+    return (u4 * u4 * u).astype(jnp.bfloat16)
+
+
+def decode(coded, scale):
+    w = coded.astype(F32)
+    size = jnp.exp(jnp.log(jnp.abs(w)) * (1.0 / 9.0)) * scale
+    return jnp.where(w < 0, -size, size)
+
+
 def kernel(
     Z, R, entries,
     g, m_in, f_in, s_in,
     W, M, F, Q,
-    mine, swapped, S, RA, RB, R2, R3, V, N,
+    L, swapped, S, EA, EB, E2, E3, RA, RB, R2, R3, V, N, B,
     load_sem, state_sem,
-    g_sem, a1_sem, b1_sem, a2_sem, b2_sem, z_sem, n_sem, v_sem,
+    g_sem, a1_sem, b1_sem, a2_sem, b2_sem, z_sem, n_sem, m_sem, v_sem,
     gz_sem, ga_sem, gb_sem, ha_sem, hb_sem, gc_sem,
 ):
     D = 2 * Z
@@ -45,7 +59,6 @@
     d, r = lax.axis_index("dp"), lax.axis_index("rep")
     z, y = d // 2, d % 2
     x, c = r // 2, r % 2
-    me = d * R + r
     C, G = PIECES * Z, W_PIECES * Z
     to_x = (d, (1 - x) * 2 + c)
     to_y = (z * 2 + 1 - y, r)
@@ -60,6 +73,18 @@
             device_id=device, device_id_type=MESH,
         )
 
+    def peer(k, sign):
+        zz = (z + Z + sign * (k // 8)) % Z
+        return zz, (y + k // 4) % 2, (x + k // 2) % 2, (c + k) % 2
+
+    def to_peer(ref, sems, k):
+        zz, yy, xx, cc = peer(k, 1)
+        return push(ref.at[z, y, x, c], ref.at[z, y, x, c], sems, (k,), (zz * 2 + yy, xx * 2 + cc))
+
+    def from_peer(ref, sems, k):
+        zz, yy, xx, cc = peer(k, -1)
+        return push(ref.at[zz, yy, xx, cc], ref.at[zz, yy, xx, cc], sems, (k,), (zz * 2 + yy, xx * 2 + cc))
+
     def dest(k):
         return (z + 1 + k) % Z
 
@@ -75,12 +100,12 @@
 
     @pl.loop(1, n)
     def _(k):
-        t = (me + k) % n
-        pl.semaphore_signal(barrier, inc=1, device_id=(t // R, t % R), device_id_type=MESH)
+        zz, yy, xx, cc = peer(k, 1)
+        pl.semaphore_signal(barrier, inc=1, device_id=(zz * 2 + yy, xx * 2 + cc), device_id_type=MESH)
 
     def load(k):
         return pltpu.make_async_copy(
-            g.at[dest(k // PIECES), :, c, :, :, :, cols(k)], mine.at[k // PIECES, :, :, :, :, cols(k)], load_sem.at[k]
+            g.at[dest(k // PIECES), :, :, :, :, :, cols(k)], L.at[k // PIECES, :, :, :, :, :, cols(k)], load_sem.at[k]
         )
 
     @pl.loop(0, C)
@@ -93,11 +118,25 @@
     ]
     for copy in states:
         copy.start()
+
+    B[z, y, x, c] = jnp.zeros((1, 128), F32)
+
+    @pl.loop(0, C)
+    def _(k):
+        load(k).wait()
+        size = jnp.abs(L[k // PIECES, :, :, :, :, :, cols(k)].astype(F32))
+        lanes = jnp.max(size.reshape(-1, size.shape[-1]), axis=0, keepdims=True)
+        best = B[z, y, x, c]
+        for i in range(0, size.shape[-1], 128):
+            best = jnp.maximum(best, lanes[:, i : i + 128])
+        B[z, y, x, c] = best
+
     pl.semaphore_wait(barrier, n - 1)
+    to_peer(B, m_sem, 1).start()
 
     def swap(k):
         return push(
-            g.at[dest(k // PIECES), :, 1 - c, :, :, :, cols(k)], swapped.at[k // PIECES, :, :, :, :, cols(k)],
+            L.at[k // PIECES, :, 1 - c, :, :, :, cols(k)], swapped.at[k // PIECES, :, :, :, :, cols(k)],
             g_sem, (k,), to_c,
         )
 
@@ -105,48 +144,88 @@
     def _(k):
         swap(k).start()
 
+    @pl.loop(2, n)
+    def _(k):
+        to_peer(B, m_sem, k).start()
+
+    def bound(rows):
+        lanes = jnp.sum(rows.reshape(-1, 128), axis=0, keepdims=True)
+        return jnp.maximum(jnp.max(lanes), 1e-30)
+
     def first_a(k):
         i, p = k // PIECES, cols(k)
-        return push(S.at[i, :, 1 - x, 0, :, p], RA.at[i, :, :, p], a1_sem, (k,), to_x)
+        return push(EA.at[i, :, :, p], RA.at[i, :, :, p], a1_sem, (k,), to_x)
 
     def first_b(k):
         i, p = k // PIECES, cols(k)
-        return push(S.at[i, 1 - y, :, 1, :, p], RB.at[i, :, :, p], b1_sem, (k,), to_y)
+        return push(EB.at[i, :, :, p], RB.at[i, :, :, p], b1_sem, (k,), to_y)
 
     def second_a(k):
         i, p = k // PIECES, cols(k)
-        return push(S.at[i, 1 - y, x, 0, :, p], R2.at[i, 0, :, p], a2_sem, (k,), to_y)
+        return push(E2.at[i, 0, :, p], R2.at[i, 0, :, p], a2_sem, (k,), to_y)
 
     def second_b(k):
         i, p = k // PIECES, cols(k)
-        return push(S.at[i, y, 1 - x, 1, :, p], R2.at[i, 1, :, p], b2_sem, (k,), to_x)
+        return push(E2.at[i, 1, :, p], R2.at[i, 1, :, p], b2_sem, (k,), to_x)
 
     def along_z(k):
         i, p = k // PIECES, cols(k)
-        return push(S.at[i, y, x, :, :, p], R3.at[i, :, :, p], z_sem, (k,), to_z(dest(i)))
-
-    @pl.loop(0, C + TRAIL[1])
+        return push(E3.at[i, :, :, p], R3.at[i, :, :, p], z_sem, (k,), to_z(dest(i)))
+
+    from_peer(B, m_sem, 1).wait_recv()
+    own_bound = bound(B[z, y, x])
+    own_scale = TOP / own_bound
+
+    def stage1(k):
+        i, p = k // PIECES, cols(k)
+        swap(k).wait_recv()
+
+        def pair(yy, xx, h):
+            return L[i, yy, c, xx, h, :, p].astype(F32) + swapped[i, yy, xx, h, :, p].astype(F32)
+
+        for yy in range(2):
+            EA[i, yy, :, p] = encode(pair(yy, 1 - x, 0), own_scale)
+        first_a(k).start()
+        for xx in range(2):
+            EB[i, xx, :, p] = encode(pair(1 - y, xx, 1), own_scale)
+        first_b(k).start()
+        for j in range(2):
+            S[i, j, x, 0, :, p] = pair(j, x, 0)
+            S[i, y, j, 1, :, p] = pair(y, j, 1)
+
+    @pl.loop(0, TRAIL[0])
+    def _(step):
+        stage1(step)
+
+    @pl.loop(2, n)
+    def _(k):
+        from_peer(B, m_sem, k).wait_recv()
+
+    x_back = bound(B[z, y, 1 - x]) / TOP
+    y_back = bound(B[z, 1 - y, x]) / TOP
+    plane_bound = bound(B[z])
+    plane_scale, plane_back = TOP / plane_bound, plane_bound / TOP
+    whole_bound = bound(B[...])
+    whole_scale, whole_back = TOP / whole_bound, whole_bound / TOP
+
+    @pl.loop(TRAIL[0], C + TRAIL[1])
     def _(step):
         @pl.when(step < C)
         def _():
-            k = step
-            i, p = k // PIECES, cols(k)
-            load(k).wait()
-            swap(k).wait_recv()
-            S[i, :, :, :, :, p] = mine[i, :, :, :, :, p].astype(F32) + swapped[i, :, :, :, :, p].astype(F32)
-            first_a(k).start()
-            first_b(k).start()
-
-        @pl.when((step >= TRAIL[0]) & (step < C + TRAIL[0]))
+            stage1(step)
+
+        @pl.when(step < C + TRAIL[0])
         def _():
             k = step - TRAIL[0]
             i, p = k // PIECES, cols(k)
             first_a(k).wait_recv()
-            S[i, :, x, 0, :, p] = S[i, :, x, 0, :, p] + RA[i, :, :, p]
+            E2[i, 0, :, p] = encode(S[i, 1 - y, x, 0, :, p] + decode(RA[i, 1 - y, :, p], x_back), plane_scale)
             second_a(k).start()
             first_b(k).wait_recv()
-            S[i, y, :, 1, :, p] = S[i, y, :, 1, :, p] + RB[i, :, :, p]
+            E2[i, 1, :, p] = encode(S[i, y, 1 - x, 1, :, p] + decode(RB[i, 1 - x, :, p], y_back), plane_scale)
             second_b(k).start()
+            S[i, y, x, 0, :, p] = S[i, y, x, 0, :, p] + decode(RA[i, y, :, p], x_back)
+            S[i, y, x, 1, :, p] = S[i, y, x, 1, :, p] + decode(RB[i, x, :, p], y_back)
 
         @pl.when(step >= TRAIL[1])
         def _():
@@ -154,34 +233,31 @@
             i, p = k // PIECES, cols(k)
             second_a(k).wait_recv()
             second_b(k).wait_recv()
-            S[i, y, x, :, :, p] = S[i, y, x, :, :, p] + R2[i, :, :, p]
+            both = S[i, y, x, :, :, p] + decode(R2[i, :, :, p], plane_back)
 
             @pl.when(k < C - PIECES)
             def _():
+                E3[i, :, :, p] = encode(both, whole_scale)
                 along_z(k).start()
 
+            @pl.when(k >= C - PIECES)
+            def _():
+                S[i, y, x, :, :, p] = both
+
     @pl.loop(0, C - PIECES)
     def _(k):
         i, p = k // PIECES, cols(k)
         along_z(k).wait_recv()
-        S[Z - 1, y, x, :, :, p] = S[Z - 1, y, x, :, :, p] + R3[i, :, :, p]
+        S[Z - 1, y, x, :, :, p] = S[Z - 1, y, x, :, :, p] + decode(R3[i, :, :, p], whole_back)
 
     total = S[Z - 1, y, x]
     V[c, x] = total
     lanes = jnp.sum((total * total).reshape(-1, total.shape[-1]), axis=0, keepdims=True)
-    N[me] = sum(lanes[:, i : i + 128] for i in range(0, total.shape[-1], 128))
-
-    def norm_part(k):
-        t = (me + k) % n
-        return push(N.at[me], N.at[me], n_sem, (k,), (t // R, t % R))
-
-    def norm_recv(k):
-        t = (me + n - k) % n
-        return push(N.at[t], N.at[t], n_sem, (k,), (t // R, t % R))
+    N[z, y, x, c] = sum(lanes[:, i : i + 128] for i in range(0, total.shape[-1], 128))
 
     @pl.loop(1, n)
     def _(k):
-        norm_part(k).start()
+        to_peer(N, n_sem, n - k).start()
 
     v_x = push(V.at[c, x], V.at[c, x], v_sem, (0,), to_x)
     v_c = push(V.at[c, x], V.at[c, x], v_sem, (1,), to_c)
@@ -197,7 +273,7 @@
 
     @pl.loop(1, n)
     def _(k):
-        norm_recv(k).wait_recv()
+        from_peer(N, n_sem, k).wait_recv()
 
     factor = clip_factor(jnp.sum(N[...]), entries)
 
@@ -206,9 +282,9 @@
         M[cc, xx] = new_master
         F[cc, xx] = new_first
         Q[cc, xx] = new_second
-        return new_master
-
-    W[z, y, c, x] = update(c, x).astype(jnp.bfloat16)
+        W[z, y, cc, xx] = new_master.astype(jnp.bfloat16)
+
+    update(c, x)
 
     def source(b):
         return (z + Z - b // W_PIECES) % Z
@@ -221,31 +297,55 @@
         block = W.at[source(j + W_PIECES), y, c, x, :, :, w_cols(j)]
         return push(block, block, gz_sem, (j,), to_z(dest(j // W_PIECES)))
 
+    def same(ref, sems, b, device):
+        return push(ref, ref, sems, (b,), device)
+
+    def own_a(b, yy):
+        return same(W.at[z, yy, c, x, :, :, w_cols(b)], ga_sem, b, to_y)
+
+    def own_h(b, xx):
+        return same(W.at[z, 1 - y, c, xx, :, :, w_cols(b)], ha_sem, b, to_x)
+
+    def own_c(b, cc):
+        return same(W.at[z, 1 - y, cc, :, :, :, w_cols(b)], gc_sem, b, to_c)
+
+    def ga(b, yy):
+        return same(W.at[source(b), yy, c, x, 0, :, w_cols(b)], ga_sem, b, to_y)
+
+    def gb(b, xx):
+        return same(W.at[source(b), y, c, xx, 1, :, w_cols(b)], gb_sem, b, to_x)
+
+    def ha(b, xx):
+        return same(W.at[source(b), :, c, xx, 0, :, w_cols(b)], ha_sem, b, to_x)
+
+    def hb(b, yy):
+        return same(W.at[source(b), yy, c, :, 1, :, w_cols(b)], hb_sem, b, to_y)
+
+    def gc(b, cc):
+        return same(W.at[source(b), :, cc, :, :, :, w_cols(b)], gc_sem, b, to_c)
+
+    @pl.loop(0, W_PIECES)
+    def _(b):
+        own_a(b, y).start()
+
     @pl.loop(0, G - W_PIECES)
     def _(j):
         gather_z(j).start()
 
-    def same(ref, sems, b, device):
-        return push(ref, ref, sems, (b,), device)
-
-    def ga(b, yy):
-        return same(W.at[source(b), yy, c, x, 0, :, w_cols(b)], ga_sem, b, to_y)
-
-    def gb(b, xx):
-        return same(W.at[source(b), y, c, xx, 1, :, w_cols(b)], gb_sem, b, to_x)
-
-    def ha(b, xx):
-        return same(W.at[source(b), :, c, xx, 0, :, w_cols(b)], ha_sem, b, to_x)
-
-    def hb(b, yy):
-        return same(W.at[source(b), yy, c, :, 1, :, w_cols(b)], hb_sem, b, to_y)
-
-    def gc(b, cc):
-        return same(W.at[source(b), :, cc, :, :, :, w_cols(b)], gc_sem, b, to_c)
-
-    @pl.loop(0, G + W_TRAIL[1])
+    got_x.wait_recv()
+    v_xc.start()
+    update(c, 1 - x)
+    got_c.wait_recv()
+    update(1 - c, x)
+
+    @pl.loop(0, W_PIECES)
+    def _(b):
+        own_a(b, 1 - y).wait_recv()
+        own_h(b, x).start()
+
+    @pl.loop(W_PIECES, G + W_TRAIL[1])
     def _(step):
-        @pl.when((step >= W_TRAIL[0]) & (step < G + W_TRAIL[0]))
+        @pl.when((step >= W_PIECES + W_TRAIL[0]) & (step < G + W_TRAIL[0]))
         def _():
             b = step - W_TRAIL[0]
             ga(b, 1 - y).wait_recv()
@@ -256,38 +356,32 @@
         @pl.when(step < G)
         def _():
             b = step
-
-            @pl.when(b >= W_PIECES)
-            def _():
-                got_z(b - W_PIECES).wait_recv()
-
+            got_z(b - W_PIECES).wait_recv()
             ga(b, y).start()
             gb(b, x).start()
 
-        @pl.when(step == 1)
-        def _():
-            got_x.wait_recv()
-            v_xc.start()
-            update(c, 1 - x)
-
-        @pl.when(step == 2)
-        def _():
-            got_c.wait_recv()
-            update(1 - c, x)
-
-        @pl.when(step == 3)
+        @pl.when(step == W_PIECES)
         def _():
             got_xc.wait_recv()
             update(1 - c, 1 - x)
 
-        @pl.when(step >= W_TRAIL[1])
+            @pl.loop(0, W_PIECES)
+            def _(b):
+                own_h(b, 1 - x).wait_recv()
+                own_c(b, c).start()
+
+        @pl.when(step >= W_PIECES + W_TRAIL[1])
         def _():
             b = step - W_TRAIL[1]
             ha(b, 1 - x).wait_recv()
             hb(b, 1 - y).wait_recv()
             gc(b, c).start()
 
-    @pl.loop(0, G)
+    @pl.loop(0, W_PIECES)
+    def _(b):
+        own_c(b, 1 - c).wait_recv()
+
+    @pl.loop(W_PIECES, G)
     def _(b):
         gc(b, 1 - c).wait_recv()
 
@@ -297,7 +391,8 @@
 
     @pl.loop(1, n)
     def _(k):
-        norm_part(k).wait_send()
+        to_peer(B, m_sem, k).wait_send()
+        to_peer(N, n_sem, k).wait_send()
 
     @pl.loop(0, C)
     def _(k):
@@ -311,7 +406,13 @@
     def _(k):
         along_z(k).wait_send()
 
-    @pl.loop(0, G)
+    @pl.loop(0, W_PIECES)
+    def _(b):
+        own_a(b, y).wait_send()
+        own_h(b, x).wait_send()
+        own_c(b, c).wait_send()
+
+    @pl.loop(W_PIECES, G)
     def _(b):
         ga(b, y).wait_send()
         gb(b, x).wait_send()
@@ -350,19 +451,24 @@
         in_specs=[hbm] * 4,
         out_specs=[vmem] * 4,
         scratch_shapes=[
-            pltpu.VMEM((Z,) + part, bf16),
+            pltpu.VMEM((Z, 2) + part, bf16),
             pltpu.VMEM((Z,) + part, bf16),
             pltpu.VMEM((Z,) + part, F32),
-            pltpu.VMEM((Z, 2, t, cols), F32),
-            pltpu.VMEM((Z, 2, t, cols), F32),
-            pltpu.VMEM((Z, 2, t, cols), F32),
-            pltpu.VMEM((Z - 1, 2, t, cols), F32),
+            pltpu.VMEM((Z, 2, t, cols), bf16),
+            pltpu.VMEM((Z, 2, t, cols), bf16),
+            pltpu.VMEM((Z, 2, t, cols), bf16),
+            pltpu.VMEM((Z - 1, 2, t, cols), bf16),
+            pltpu.VMEM((Z, 2, t, cols), bf16),
+            pltpu.VMEM((Z, 2, t, cols), bf16),
+            pltpu.VMEM((Z, 2, t, cols), bf16),
+            pltpu.VMEM((Z - 1, 2, t, cols), bf16),
             pltpu.VMEM(part, F32),
-            pltpu.VMEM((n, 1, 128), F32),
+            pltpu.VMEM((Z, 2, 2, 2, 1, 128), F32),
+            pltpu.VMEM((Z, 2, 2, 2, 1, 128), F32),
             dma((PIECES * Z,)), dma((3,)),
             dma((2, PIECES * Z)), dma((2, PIECES * Z)), dma((2, PIECES * Z)),
             dma((2, PIECES * Z)), dma((2, PIECES * Z)), dma((2, PIECES * Z)),
-            dma((2, n)), dma((2, 3)),
+            dma((2, n)), dma((2, n)), dma((2, 3)),
             dma((2, W_PIECES * Z)), dma((2, W_PIECES * Z)), dma((2, W_PIECES * Z)),
             dma((2, W_PIECES * Z)), dma((2, W_PIECES * Z)), dma((2, W_PIECES * Z)),
         ],

time: 83.5 us -> 68.7 us (0.82)
  Pallas kernels: 82.6 us -> 67.9 us
    pallas_call x1, Pallas kernels: 79.6 us -> 64.9 us  [body(): pl.pallas_call(functools.partial(kernel, Z, R, rows * cols), out_shape=[p...]
where the time goes in v1:
time: 68.7 us; the launch traced here: 68.6 us
  Pallas kernels  67.9 us (99%)
    pallas_call x1, Pallas kernels, body(): pl.pallas_call(functools.partial(kernel, Z, R, rows * cols), out_shape=[p...  64.9 us
    pallas_call x1, Pallas kernels, body(): pl.pallas_call(write_out, out_shape=[jax.ShapeDtypeStruct(*shape) for sha...  3.02 us

profile of v1, /device:TPU:1, one launch (start us, length us, event | category | flops | bytes accessed | tf_op | source)
XLA Modules:
  0.0 68.6 jit_solution(3481103937133830808)
XLA Ops:
  0.6 64.9 %shard_map.75 = (bf16[4,2,2,2,2,64,512]{6,5,4,3,2,1,0:T(8,128)(2,1)S(1)}, f32[2,2,2,64,512]{4,3,2,1,0:T(8,128)S(1)}, f32[2,2,2,64,512]{4,3,2,1,0:T(8,128)S(1)}, f32[2,2,2,64,512]{4,3,2,1,0:T(8,128)S(1)}) custom-call(bf16[4,2,2,2,2,64,512]{6,5,4,3,2,1,0:T(8,128)(2,1)} %bitcast.8, f32[2,2,2,64,512]{4,3,2,1,0:T(8,128)} %bitcast.9, ...), custom_call_target="tpu_custom_call" | custom-call | tf_op jit(solution)/shard_map/pallas_call | solution.py:448
  65.5 3.0 %shard_map.76 = (bf16[4,2,2,2,2,64,512]{6,5,4,3,2,1,0:T(8,128)(2,1)}, f32[2,2,2,64,512]{4,3,2,1,0:T(8,128)}, f32[2,2,2,64,512]{4,3,2,1,0:T(8,128)}, f32[2,2,2,64,512]{4,3,2,1,0:T(8,128)}) custom-call(bf16[4,2,2,2,2,64,512]{6,5,4,3,2,1,0:T(8,128)(2,1)S(1)} %get-tuple-element.12.refs_0_, f32[2,2,2,64,512]{4,3,2,1,0:T(8,128)S(1)} %get-tuple-element.13.refs_1_, ...), custom_call_target="tpu_custom_call" | custom-call | tf_op jit(solution)/shard_map/pallas_call | solution.py:482

commit v2 on v1

--- a/solution.py
+++ b/solution.py
@@ -15,6 +15,7 @@
 W_PIECES, W_TRAIL = 2, (2, 3)
 VMEM_BYTES = 63 * 1024 * 1024
 TOP = 2.0**14
+OWN, CORE, CHIP, FROM_X, FROM_Y, PAIR, PAIR_Y, PLANE, BELOW, UP, ABOVE, DOWN = range(12)
 
 
 def adam_update(clipped, master, first_moment, second_moment):
@@ -49,10 +50,10 @@
     Z, R, entries,
     g, m_in, f_in, s_in,
     W, M, F, Q,
-    L, swapped, S, EA, EB, E2, E3, RA, RB, R2, R3, V, N, B,
+    L, swapped, S, EA, EB, E2, E3, RA, RB, R2, RU, RD, V, N, B,
     load_sem, state_sem,
-    g_sem, a1_sem, b1_sem, a2_sem, b2_sem, z_sem, n_sem, m_sem, v_sem,
-    gz_sem, ga_sem, gb_sem, ha_sem, hb_sem, gc_sem,
+    g_sem, a1_sem, b1_sem, a2_sem, b2_sem, zu_sem, zd_sem, n_sem, m_sem, v_sem,
+    gu_sem, gd_sem, ga_sem, gb_sem, ha_sem, hb_sem, gc_sem,
 ):
     D = 2 * Z
     n = D * R
@@ -85,8 +86,16 @@
         zz, yy, xx, cc = peer(k, -1)
         return push(ref.at[zz, yy, xx, cc], ref.at[zz, yy, xx, cc], sems, (k,), (zz * 2 + yy, xx * 2 + cc))
 
+    below, above = z, Z - 1 - z
+    near = jnp.minimum(below, above)
+
+    def nth(j):
+        paired = jnp.where(j % 2 == 1, z + (j + 1) // 2, z - (j + 1) // 2)
+        single = jnp.where(below < above, z + j - near, z - j + near)
+        return jnp.where(j <= 2 * near, paired, single)
+
     def dest(k):
-        return (z + 1 + k) % Z
+        return nth(Z - 1 - k)
 
     def cols(q):
         width = g.shape[-1] // PIECES
@@ -96,12 +105,19 @@
         width = g.shape[-1] // W_PIECES
         return pl.ds(pl.multiple_of((q % W_PIECES) * width, width), width)
 
+    B[...] = jnp.zeros(B.shape, F32)
     barrier = pltpu.get_barrier_semaphore()
 
-    @pl.loop(1, n)
-    def _(k):
-        zz, yy, xx, cc = peer(k, 1)
-        pl.semaphore_signal(barrier, inc=1, device_id=(zz * 2 + yy, xx * 2 + cc), device_id_type=MESH)
+    for device in (to_c, to_x, to_y):
+        pl.semaphore_signal(barrier, inc=1, device_id=device, device_id_type=MESH)
+
+    @pl.when(below > 0)
+    def _():
+        pl.semaphore_signal(barrier, inc=1, device_id=to_z(z - 1), device_id_type=MESH)
+
+    @pl.when(above > 0)
+    def _():
+        pl.semaphore_signal(barrier, inc=1, device_id=to_z(z + 1), device_id_type=MESH)
 
     def load(k):
         return pltpu.make_async_copy(
@@ -119,20 +135,25 @@
     for copy in states:
         copy.start()
 
-    B[z, y, x, c] = jnp.zeros((1, 128), F32)
-
     @pl.loop(0, C)
     def _(k):
         load(k).wait()
         size = jnp.abs(L[k // PIECES, :, :, :, :, :, cols(k)].astype(F32))
         lanes = jnp.max(size.reshape(-1, size.shape[-1]), axis=0, keepdims=True)
-        best = B[z, y, x, c]
+        best = B[OWN]
         for i in range(0, size.shape[-1], 128):
             best = jnp.maximum(best, lanes[:, i : i + 128])
-        B[z, y, x, c] = best
-
-    pl.semaphore_wait(barrier, n - 1)
-    to_peer(B, m_sem, 1).start()
+        B[OWN] = best
+
+    pl.semaphore_wait(barrier, 3 + jnp.minimum(below, 1) + jnp.minimum(above, 1))
+
+    def row(source, target, device):
+        return push(B.at[source], B.at[target], m_sem, (target,), device)
+
+    to_core = row(OWN, CORE, to_c)
+    chip_x, chip_y = row(CHIP, FROM_X, to_x), row(CHIP, FROM_Y, to_y)
+    pair_y = row(PAIR, PAIR_Y, to_y)
+    row_up, row_down = row(UP, BELOW, to_z(z + 1)), row(DOWN, ABOVE, to_z(z - 1))
 
     def swap(k):
         return push(
@@ -144,13 +165,10 @@
     def _(k):
         swap(k).start()
 
-    @pl.loop(2, n)
-    def _(k):
-        to_peer(B, m_sem, k).start()
-
-    def bound(rows):
-        lanes = jnp.sum(rows.reshape(-1, 128), axis=0, keepdims=True)
-        return jnp.maximum(jnp.max(lanes), 1e-30)
+    to_core.start()
+
+    def bound(index):
+        return jnp.maximum(jnp.max(B[index]), 1e-30)
 
     def first_a(k):
         i, p = k // PIECES, cols(k)
@@ -168,13 +186,21 @@
         i, p = k // PIECES, cols(k)
         return push(E2.at[i, 1, :, p], R2.at[i, 1, :, p], b2_sem, (k,), to_x)
 
-    def along_z(k):
+    def z_up(k):
         i, p = k // PIECES, cols(k)
-        return push(E3.at[i, :, :, p], R3.at[i, :, :, p], z_sem, (k,), to_z(dest(i)))
-
-    from_peer(B, m_sem, 1).wait_recv()
-    own_bound = bound(B[z, y, x])
-    own_scale = TOP / own_bound
+        q = dest(i)
+        return push(E3.at[i, :, :, p], RU.at[q, :, :, p], zu_sem, (q * PIECES + k % PIECES,), to_z(z + 1))
+
+    def z_down(k):
+        i, p = k // PIECES, cols(k)
+        q = dest(i)
+        return push(E3.at[i, :, :, p], RD.at[q, :, :, p], zd_sem, (q * PIECES + k % PIECES,), to_z(z - 1))
+
+    to_core.wait_recv()
+    B[CHIP] = B[OWN] + B[CORE]
+    chip_x.start()
+    chip_y.start()
+    own_scale = TOP / bound(CHIP)
 
     def stage1(k):
         i, p = k // PIECES, cols(k)
@@ -197,18 +223,20 @@
     def _(step):
         stage1(step)
 
-    @pl.loop(2, n)
-    def _(k):
-        from_peer(B, m_sem, k).wait_recv()
-
-    x_back = bound(B[z, y, 1 - x]) / TOP
-    y_back = bound(B[z, 1 - y, x]) / TOP
-    plane_bound = bound(B[z])
+    chip_x.wait_recv()
+    B[PAIR] = B[CHIP] + B[FROM_X]
+    pair_y.start()
+    chip_y.wait_recv()
+    x_back, y_back = bound(FROM_X) / TOP, bound(FROM_Y) / TOP
+    pair_y.wait_recv()
+    B[PLANE] = B[PAIR] + B[PAIR_Y]
+    plane_bound = bound(PLANE)
     plane_scale, plane_back = TOP / plane_bound, plane_bound / TOP
-    whole_bound = bound(B[...])
-    whole_scale, whole_back = TOP / whole_bound, whole_bound / TOP
-
-    @pl.loop(TRAIL[0], C + TRAIL[1])
+
+    hop = 1 if Z <= 4 else Z
+    up_lag, down_lag = jnp.minimum(below, hop), jnp.minimum(above, hop)
+
+    @pl.loop(TRAIL[0], C + TRAIL[1] + max(0, min(hop, Z - 1) - PIECES))
     def _(step):
         @pl.when(step < C)
         def _():
@@ -227,28 +255,76 @@
             S[i, y, x, 0, :, p] = S[i, y, x, 0, :, p] + decode(RA[i, y, :, p], x_back)
             S[i, y, x, 1, :, p] = S[i, y, x, 1, :, p] + decode(RB[i, x, :, p], y_back)
 
-        @pl.when(step >= TRAIL[1])
+        @pl.when(step == TRAIL[0] + below)
+        def _():
+            @pl.when(below > 0)
+            def _():
+                row_up.wait_recv()
+
+            B[UP] = B[PLANE] + B[BELOW]
+
+            @pl.when(above > 0)
+            def _():
+                row_up.start()
+
+        @pl.when(step == TRAIL[0] + above)
+        def _():
+            @pl.when(above > 0)
+            def _():
+                row_down.wait_recv()
+
+            B[DOWN] = B[PLANE] + B[ABOVE]
+
+            @pl.when(below > 0)
+            def _():
+                row_down.start()
+
+        @pl.when((step >= TRAIL[1]) & (step < C + TRAIL[1]))
         def _():
             k = step - TRAIL[1]
             i, p = k // PIECES, cols(k)
             second_a(k).wait_recv()
             second_b(k).wait_recv()
-            both = S[i, y, x, :, :, p] + decode(R2[i, :, :, p], plane_back)
-
-            @pl.when(k < C - PIECES)
-            def _():
-                E3[i, :, :, p] = encode(both, whole_scale)
-                along_z(k).start()
-
-            @pl.when(k >= C - PIECES)
-            def _():
-                S[i, y, x, :, :, p] = both
-
-    @pl.loop(0, C - PIECES)
-    def _(k):
-        i, p = k // PIECES, cols(k)
-        along_z(k).wait_recv()
-        S[Z - 1, y, x, :, :, p] = S[Z - 1, y, x, :, :, p] + decode(R3[i, :, :, p], whole_back)
+            S[i, y, x, :, :, p] = S[i, y, x, :, :, p] + decode(R2[i, :, :, p], plane_back)
+
+        def relay(lag, side, arrow, received, came, sent):
+            k = jnp.clip(step - TRAIL[1] - lag, 0, C - PIECES - 1)
+            i, p = k // PIECES, cols(k)
+            q = dest(i)
+
+            @pl.when((k == step - TRAIL[1] - lag) & ((q > z) if arrow is z_up else (q < z)))
+            def _():
+                scale = TOP / bound(sent)
+
+                @pl.when(side > 0)
+                def _():
+                    arrow(k).wait_recv()
+                    value = S[i, y, x, :, :, p] + decode(received[q, :, :, p], bound(came) / TOP)
+                    E3[i, :, :, p] = encode(value, scale)
+
+                @pl.when(side == 0)
+                def _():
+                    E3[i, :, :, p] = encode(S[i, y, x, :, :, p], scale)
+
+                arrow(k).start()
+
+        relay(up_lag, below, z_up, RU, BELOW, UP)
+        relay(down_lag, above, z_down, RD, ABOVE, DOWN)
+
+    def last(arrow, received, came):
+        @pl.loop(C - PIECES, C)
+        def _(k):
+            p = cols(k)
+            arrow(k).wait_recv()
+            S[Z - 1, y, x, :, :, p] = S[Z - 1, y, x, :, :, p] + decode(received[z, :, :, p], bound(came) / TOP)
+
+    @pl.when(below > 0)
+    def _():
+        last(z_up, RU, BELOW)
+
+    @pl.when(above > 0)
+    def _():
+        last(z_down, RD, ABOVE)
 
     total = S[Z - 1, y, x]
     V[c, x] = total
@@ -277,25 +353,26 @@
 
     factor = clip_factor(jnp.sum(N[...]), entries)
 
-    def update(cc, xx):
-        new_master, new_first, new_second = adam_update(factor * V[cc, xx], M[cc, xx], F[cc, xx], Q[cc, xx])
-        M[cc, xx] = new_master
-        F[cc, xx] = new_first
-        Q[cc, xx] = new_second
-        W[z, y, cc, xx] = new_master.astype(jnp.bfloat16)
-
-    update(c, x)
+    def update(cc, xx, p):
+        at = (cc, xx, slice(None), slice(None), p)
+        new_master, new_first, new_second = adam_update(factor * V[at], M[at], F[at], Q[at])
+        M[at] = new_master
+        F[at] = new_first
+        Q[at] = new_second
+        W[(z, y) + at] = new_master.astype(jnp.bfloat16)
+
+    every = slice(None)
 
     def source(b):
-        return (z + Z - b // W_PIECES) % Z
-
-    def gather_z(j):
-        block = W.at[z, y, c, x, :, :, w_cols(j)]
-        return push(block, block, gz_sem, (j,), to_z(dest(j // W_PIECES)))
-
-    def got_z(j):
-        block = W.at[source(j + W_PIECES), y, c, x, :, :, w_cols(j)]
-        return push(block, block, gz_sem, (j,), to_z(dest(j // W_PIECES)))
+        return nth(b // W_PIECES)
+
+    def lift(s, b):
+        block = W.at[s, y, c, x, :, :, w_cols(b)]
+        return push(block, block, gu_sem, (s * W_PIECES + b % W_PIECES,), to_z(z + 1))
+
+    def drop(s, b):
+        block = W.at[s, y, c, x, :, :, w_cols(b)]
+        return push(block, block, gd_sem, (s * W_PIECES + b % W_PIECES,), to_z(z - 1))
 
     def same(ref, sems, b, device):
         return push(ref, ref, sems, (b,), device)
@@ -326,17 +403,22 @@
 
     @pl.loop(0, W_PIECES)
     def _(b):
+        update(c, x, w_cols(b))
         own_a(b, y).start()
 
-    @pl.loop(0, G - W_PIECES)
-    def _(j):
-        gather_z(j).start()
+        @pl.when(above > 0)
+        def _():
+            lift(z, b).start()
+
+        @pl.when(below > 0)
+        def _():
+            drop(z, b).start()
 
     got_x.wait_recv()
     v_xc.start()
-    update(c, 1 - x)
+    update(c, 1 - x, every)
     got_c.wait_recv()
-    update(1 - c, x)
+    update(1 - c, x, every)
 
     @pl.loop(0, W_PIECES)
     def _(b):
@@ -356,14 +438,31 @@
         @pl.when(step < G)
         def _():
             b = step
-            got_z(b - W_PIECES).wait_recv()
+            far = b // W_PIECES
+
+            @pl.when(far <= below)
+            def _():
+                lift(z - far, b).wait_recv()
+
+                @pl.when(above > 0)
+                def _():
+                    lift(z - far, b).start()
+
+            @pl.when(far <= above)
+            def _():
+                drop(z + far, b).wait_recv()
+
+                @pl.when(below > 0)
+                def _():
+                    drop(z + far, b).start()
+
             ga(b, y).start()
             gb(b, x).start()
 
         @pl.when(step == W_PIECES)
         def _():
             got_xc.wait_recv()
-            update(1 - c, 1 - x)
+            update(1 - c, 1 - x, every)
 
             @pl.loop(0, W_PIECES)
             def _(b):
@@ -389,9 +488,11 @@
     v_c.wait_send()
     v_xc.wait_send()
 
+    for copy in (to_core, chip_x, chip_y, pair_y):
+        copy.wait_send()
+
     @pl.loop(1, n)
     def _(k):
-        to_peer(B, m_sem, k).wait_send()
         to_peer(N, n_sem, k).wait_send()
 
     @pl.loop(0, C)
@@ -404,7 +505,33 @@
 
     @pl.loop(0, C - PIECES)
     def _(k):
-        along_z(k).wait_send()
+        @pl.when(dest(k // PIECES) > z)
+        def _():
+            z_up(k).wait_send()
+
+        @pl.when(dest(k // PIECES) < z)
+        def _():
+            z_down(k).wait_send()
+
+    @pl.when(above > 0)
+    def _():
+        row_up.wait_send()
+
+    @pl.when(below > 0)
+    def _():
+        row_down.wait_send()
+
+    @pl.loop(0, W_PIECES)
+    def _(b):
+        @pl.loop(0, Z)
+        def _(s):
+            @pl.when((s <= z) & (above > 0))
+            def _():
+                lift(s, b).wait_send()
+
+            @pl.when((s >= z) & (below > 0))
+            def _():
+                drop(s, b).wait_send()
 
     @pl.loop(0, W_PIECES)
     def _(b):
@@ -419,10 +546,6 @@
         ha(b, x).wait_send()
         hb(b, y).wait_send()
         gc(b, c).wait_send()
-
-    @pl.loop(0, G - W_PIECES)
-    def _(j):
-        gather_z(j).wait_send()
 
 
 def write_out(*refs):
@@ -457,20 +580,21 @@
             pltpu.VMEM((Z, 2, t, cols), bf16),
             pltpu.VMEM((Z, 2, t, cols), bf16),
             pltpu.VMEM((Z, 2, t, cols), bf16),
-            pltpu.VMEM((Z - 1, 2, t, cols), bf16),
-            pltpu.VMEM((Z, 2, t, cols), bf16),
-            pltpu.VMEM((Z, 2, t, cols), bf16),
-            pltpu.VMEM((Z, 2, t, cols), bf16),
-            pltpu.VMEM((Z - 1, 2, t, cols), bf16),
+            pltpu.VMEM((Z, 2, t, cols), bf16),
+            pltpu.VMEM((Z, 2, t, cols), bf16),
+            pltpu.VMEM((Z, 2, t, cols), bf16),
+            pltpu.VMEM((Z, 2, t, cols), bf16),
+            pltpu.VMEM((Z, 2, t, cols), bf16),
+            pltpu.VMEM((Z, 2, t, cols), bf16),
             pltpu.VMEM(part, F32),
             pltpu.VMEM((Z, 2, 2, 2, 1, 128), F32),
-            pltpu.VMEM((Z, 2, 2, 2, 1, 128), F32),
+            pltpu.VMEM((12, 1, 128), F32),
             dma((PIECES * Z,)), dma((3,)),
             dma((2, PIECES * Z)), dma((2, PIECES * Z)), dma((2, PIECES * Z)),
-            dma((2, PIECES * Z)), dma((2, PIECES * Z)), dma((2, PIECES * Z)),
-            dma((2, n)), dma((2, n)), dma((2, 3)),
+            dma((2, PIECES * Z)), dma((2, PIECES * Z)), dma((2, PIECES * Z)), dma((2, PIECES * Z)),
+            dma((2, n)), dma((2, 12)), dma((2, 3)),
             dma((2, W_PIECES * Z)), dma((2, W_PIECES * Z)), dma((2, W_PIECES * Z)),
-            dma((2, W_PIECES * Z)), dma((2, W_PIECES * Z)), dma((2, W_PIECES * Z)),
+            dma((2, W_PIECES * Z)), dma((2, W_PIECES * Z)), dma((2, W_PIECES * Z)), dma((2, W_PIECES * Z)),
         ],
         compiler_params=pltpu.CompilerParams(
             collective_id=0, has_side_effects=True, vmem_limit_bytes=VMEM_BYTES - held_bytes

time: 68.7 us -> 73 us (1.063)
  Pallas kernels: 67.9 us -> 72.2 us
    pallas_call x1, Pallas kernels: 64.9 us -> 69.2 us  [body(): pl.pallas_call(functools.partial(kernel, Z, R, rows * cols), out_shape=[p...]
where the time goes in v2:
time: 73 us; the launch traced here: 72.8 us
  Pallas kernels  72.2 us (99%)
    pallas_call x1, Pallas kernels, body(): pl.pallas_call(functools.partial(kernel, Z, R, rows * cols), out_shape=[p...  69.2 us
    pallas_call x1, Pallas kernels, body(): pl.pallas_call(write_out, out_shape=[jax.ShapeDtypeStruct(*shape) for sha...  3.02 us

profile of v2, /device:TPU:1, one launch (start us, length us, event | category | flops | bytes accessed | tf_op | source)
XLA Modules:
  0.0 72.8 jit_solution(10730065357092751903)
XLA Ops:
  0.6 69.2 %shard_map.75 = (bf16[4,2,2,2,2,64,512]{6,5,4,3,2,1,0:T(8,128)(2,1)S(1)}, f32[2,2,2,64,512]{4,3,2,1,0:T(8,128)S(1)}, f32[2,2,2,64,512]{4,3,2,1,0:T(8,128)S(1)}, f32[2,2,2,64,512]{4,3,2,1,0:T(8,128)S(1)}) custom-call(bf16[4,2,2,2,2,64,512]{6,5,4,3,2,1,0:T(8,128)(2,1)} %bitcast.8, f32[2,2,2,64,512]{4,3,2,1,0:T(8,128)} %bitcast.9, ...), custom_call_target="tpu_custom_call" | custom-call | tf_op jit(solution)/shard_map/pallas_call | solution.py:571
  69.8 3.0 %shard_map.76 = (bf16[4,2,2,2,2,64,512]{6,5,4,3,2,1,0:T(8,128)(2,1)}, f32[2,2,2,64,512]{4,3,2,1,0:T(8,128)}, f32[2,2,2,64,512]{4,3,2,1,0:T(8,128)}, f32[2,2,2,64,512]{4,3,2,1,0:T(8,128)}) custom-call(bf16[4,2,2,2,2,64,512]{6,5,4,3,2,1,0:T(8,128)(2,1)S(1)} %get-tuple-element.12.refs_0_, f32[2,2,2,64,512]{4,3,2,1,0:T(8,128)S(1)} %get-tuple-element.13.refs_1_, ...), custom_call_target="tpu_custom_call" | custom-call | tf_op jit(solution)/shard_map/pallas_call | solution.py:606

commit v3 on v1

--- a/solution.py
+++ b/solution.py
@@ -15,6 +15,7 @@
 W_PIECES, W_TRAIL = 2, (2, 3)
 VMEM_BYTES = 63 * 1024 * 1024
 TOP = 2.0**14
+OWN, CORE, CHIP, FROM_X, FROM_Y, ALONG_X, ALONG_Y, FAR_X, FAR_Y, PLANES = range(10)
 
 
 def adam_update(clipped, master, first_moment, second_moment):
@@ -51,7 +52,7 @@
     W, M, F, Q,
     L, swapped, S, EA, EB, E2, E3, RA, RB, R2, R3, V, N, B,
     load_sem, state_sem,
-    g_sem, a1_sem, b1_sem, a2_sem, b2_sem, z_sem, n_sem, m_sem, v_sem,
+    g_sem, a1_sem, b1_sem, a2_sem, b2_sem, z_sem, n_sem, m_sem, p_sem, t_sem, v_sem,
     gz_sem, ga_sem, gb_sem, ha_sem, hb_sem, gc_sem,
 ):
     D = 2 * Z
@@ -85,6 +86,8 @@
         zz, yy, xx, cc = peer(k, -1)
         return push(ref.at[zz, yy, xx, cc], ref.at[zz, yy, xx, cc], sems, (k,), (zz * 2 + yy, xx * 2 + cc))
 
+    below, above = z, Z - 1 - z
+
     def dest(k):
         return (z + 1 + k) % Z
 
@@ -96,12 +99,19 @@
         width = g.shape[-1] // W_PIECES
         return pl.ds(pl.multiple_of((q % W_PIECES) * width, width), width)
 
+    B[...] = jnp.zeros(B.shape, F32)
     barrier = pltpu.get_barrier_semaphore()
 
-    @pl.loop(1, n)
-    def _(k):
-        zz, yy, xx, cc = peer(k, 1)
-        pl.semaphore_signal(barrier, inc=1, device_id=(zz * 2 + yy, xx * 2 + cc), device_id_type=MESH)
+    for device in (to_c, to_x, to_y):
+        pl.semaphore_signal(barrier, inc=1, device_id=device, device_id_type=MESH)
+
+    @pl.when(below > 0)
+    def _():
+        pl.semaphore_signal(barrier, inc=1, device_id=to_z(z - 1), device_id_type=MESH)
+
+    @pl.when(above > 0)
+    def _():
+        pl.semaphore_signal(barrier, inc=1, device_id=to_z(z + 1), device_id_type=MESH)
 
     def load(k):
         return pltpu.make_async_copy(
@@ -119,20 +129,52 @@
     for copy in states:
         copy.start()
 
-    B[z, y, x, c] = jnp.zeros((1, 128), F32)
-
     @pl.loop(0, C)
     def _(k):
         load(k).wait()
         size = jnp.abs(L[k // PIECES, :, :, :, :, :, cols(k)].astype(F32))
         lanes = jnp.max(size.reshape(-1, size.shape[-1]), axis=0, keepdims=True)
-        best = B[z, y, x, c]
+        best = B[OWN]
         for i in range(0, size.shape[-1], 128):
             best = jnp.maximum(best, lanes[:, i : i + 128])
-        B[z, y, x, c] = best
-
-    pl.semaphore_wait(barrier, n - 1)
-    to_peer(B, m_sem, 1).start()
+        B[OWN] = best
+
+    pl.semaphore_wait(barrier, 3 + jnp.minimum(below, 1) + jnp.minimum(above, 1))
+
+    def row(source, target, device):
+        return push(B.at[source], B.at[target], m_sem, (target,), device)
+
+    to_core = row(OWN, CORE, to_c)
+    chip_x, chip_y = row(CHIP, FROM_X, to_x), row(CHIP, FROM_Y, to_y)
+    far_x, far_y = row(ALONG_X, FAR_X, to_y), row(ALONG_Y, FAR_Y, to_x)
+
+    def plane(k, source):
+        return push(B.at[PLANES + source], B.at[PLANES + source], p_sem, (k,), to_z(dest(k)))
+
+    to_core.start()
+
+    def chain(j):
+        @pl.when(below == j)
+        def _():
+            @pl.when(below > 0)
+            def _():
+                pl.semaphore_wait(t_sem.at[0], 1)
+
+            @pl.when(above > 0)
+            def _():
+                pl.semaphore_signal(t_sem.at[0], inc=1, device_id=to_z(z + 1), device_id_type=MESH)
+
+        @pl.when(above == j)
+        def _():
+            @pl.when(above > 0)
+            def _():
+                pl.semaphore_wait(t_sem.at[1], 1)
+
+            @pl.when(below > 0)
+            def _():
+                pl.semaphore_signal(t_sem.at[1], inc=1, device_id=to_z(z - 1), device_id_type=MESH)
+
+    chain(0)
 
     def swap(k):
         return push(
@@ -144,13 +186,8 @@
     def _(k):
         swap(k).start()
 
-    @pl.loop(2, n)
-    def _(k):
-        to_peer(B, m_sem, k).start()
-
-    def bound(rows):
-        lanes = jnp.sum(rows.reshape(-1, 128), axis=0, keepdims=True)
-        return jnp.maximum(jnp.max(lanes), 1e-30)
+    def bound(index):
+        return jnp.maximum(jnp.max(B[index]), 1e-30)
 
     def first_a(k):
         i, p = k // PIECES, cols(k)
@@ -172,9 +209,11 @@
         i, p = k // PIECES, cols(k)
         return push(E3.at[i, :, :, p], R3.at[i, :, :, p], z_sem, (k,), to_z(dest(i)))
 
-    from_peer(B, m_sem, 1).wait_recv()
-    own_bound = bound(B[z, y, x])
-    own_scale = TOP / own_bound
+    to_core.wait_recv()
+    B[CHIP] = B[OWN] + B[CORE]
+    chip_x.start()
+    chip_y.start()
+    own_scale = TOP / bound(CHIP)
 
     def stage1(k):
         i, p = k // PIECES, cols(k)
@@ -197,18 +236,47 @@
     def _(step):
         stage1(step)
 
-    @pl.loop(2, n)
-    def _(k):
-        from_peer(B, m_sem, k).wait_recv()
-
-    x_back = bound(B[z, y, 1 - x]) / TOP
-    y_back = bound(B[z, 1 - y, x]) / TOP
-    plane_bound = bound(B[z])
-    plane_scale, plane_back = TOP / plane_bound, plane_bound / TOP
-    whole_bound = bound(B[...])
-    whole_scale, whole_back = TOP / whole_bound, whole_bound / TOP
-
-    @pl.loop(TRAIL[0], C + TRAIL[1])
+    chip_x.wait_recv()
+    B[ALONG_X] = B[CHIP] + B[FROM_X]
+    far_x.start()
+    chip_y.wait_recv()
+    B[ALONG_Y] = B[CHIP] + B[FROM_Y]
+    far_y.start()
+    x_back, y_back = bound(FROM_X) / TOP, bound(FROM_Y) / TOP
+    x_scale, y_scale = TOP / bound(ALONG_X), TOP / bound(ALONG_Y)
+    chain(1)
+
+    def stage2(k):
+        i, p = k // PIECES, cols(k)
+        first_a(k).wait_recv()
+        E2[i, 0, :, p] = encode(S[i, 1 - y, x, 0, :, p] + decode(RA[i, 1 - y, :, p], x_back), x_scale)
+        second_a(k).start()
+        first_b(k).wait_recv()
+        E2[i, 1, :, p] = encode(S[i, y, 1 - x, 1, :, p] + decode(RB[i, 1 - x, :, p], y_back), y_scale)
+        second_b(k).start()
+        S[i, y, x, 0, :, p] = S[i, y, x, 0, :, p] + decode(RA[i, y, :, p], x_back)
+        S[i, y, x, 1, :, p] = S[i, y, x, 1, :, p] + decode(RB[i, x, :, p], y_back)
+
+    @pl.loop(TRAIL[0], TRAIL[1])
+    def _(step):
+        stage1(step)
+        stage2(step - TRAIL[0])
+
+    @pl.loop(2, Z)
+    def _(j):
+        chain(j)
+
+    far_x.wait_recv()
+    far_y.wait_recv()
+    B[PLANES + z] = B[ALONG_X] + B[FAR_X]
+    plane_scale = TOP / bound(PLANES + z)
+    far_x_back, far_y_back = bound(FAR_X) / TOP, bound(FAR_Y) / TOP
+
+    @pl.loop(0, Z - 1)
+    def _(k):
+        plane(k, z).start()
+
+    @pl.loop(TRAIL[1], C + TRAIL[1])
     def _(step):
         @pl.when(step < C)
         def _():
@@ -216,39 +284,37 @@
 
         @pl.when(step < C + TRAIL[0])
         def _():
-            k = step - TRAIL[0]
-            i, p = k // PIECES, cols(k)
-            first_a(k).wait_recv()
-            E2[i, 0, :, p] = encode(S[i, 1 - y, x, 0, :, p] + decode(RA[i, 1 - y, :, p], x_back), plane_scale)
-            second_a(k).start()
-            first_b(k).wait_recv()
-            E2[i, 1, :, p] = encode(S[i, y, 1 - x, 1, :, p] + decode(RB[i, 1 - x, :, p], y_back), plane_scale)
-            second_b(k).start()
-            S[i, y, x, 0, :, p] = S[i, y, x, 0, :, p] + decode(RA[i, y, :, p], x_back)
-            S[i, y, x, 1, :, p] = S[i, y, x, 1, :, p] + decode(RB[i, x, :, p], y_back)
-
-        @pl.when(step >= TRAIL[1])
-        def _():
-            k = step - TRAIL[1]
-            i, p = k // PIECES, cols(k)
-            second_a(k).wait_recv()
-            second_b(k).wait_recv()
-            both = S[i, y, x, :, :, p] + decode(R2[i, :, :, p], plane_back)
-
-            @pl.when(k < C - PIECES)
-            def _():
-                E3[i, :, :, p] = encode(both, whole_scale)
-                along_z(k).start()
-
-            @pl.when(k >= C - PIECES)
-            def _():
-                S[i, y, x, :, :, p] = both
-
-    @pl.loop(0, C - PIECES)
-    def _(k):
-        i, p = k // PIECES, cols(k)
-        along_z(k).wait_recv()
-        S[Z - 1, y, x, :, :, p] = S[Z - 1, y, x, :, :, p] + decode(R3[i, :, :, p], whole_back)
+            stage2(step - TRAIL[0])
+
+        k = step - TRAIL[1]
+        i, p = k // PIECES, cols(k)
+        second_a(k).wait_recv()
+        second_b(k).wait_recv()
+        both_a = S[i, y, x, 0, :, p] + decode(R2[i, 0, :, p], far_x_back)
+        both_b = S[i, y, x, 1, :, p] + decode(R2[i, 1, :, p], far_y_back)
+
+        @pl.when(k < C - PIECES)
+        def _():
+            E3[i, 0, :, p] = encode(both_a, plane_scale)
+            E3[i, 1, :, p] = encode(both_b, plane_scale)
+            along_z(k).start()
+
+        @pl.when(k >= C - PIECES)
+        def _():
+            S[i, y, x, 0, :, p] = both_a
+            S[i, y, x, 1, :, p] = both_b
+
+    @pl.loop(0, Z - 1)
+    def _(i):
+        source = (z + Z - 1 - i) % Z
+        plane(i, source).wait_recv()
+        back = bound(PLANES + source) / TOP
+
+        @pl.loop(0, PIECES)
+        def _(j):
+            p = cols(j)
+            along_z(i * PIECES + j).wait_recv()
+            S[Z - 1, y, x, :, :, p] = S[Z - 1, y, x, :, :, p] + decode(R3[i, :, :, p], back)
 
     total = S[Z - 1, y, x]
     V[c, x] = total
@@ -277,14 +343,15 @@
 
     factor = clip_factor(jnp.sum(N[...]), entries)
 
-    def update(cc, xx):
-        new_master, new_first, new_second = adam_update(factor * V[cc, xx], M[cc, xx], F[cc, xx], Q[cc, xx])
-        M[cc, xx] = new_master
-        F[cc, xx] = new_first
-        Q[cc, xx] = new_second
-        W[z, y, cc, xx] = new_master.astype(jnp.bfloat16)
-
-    update(c, x)
+    def update(cc, xx, p):
+        at = (cc, xx, slice(None), slice(None), p)
+        new_master, new_first, new_second = adam_update(factor * V[at], M[at], F[at], Q[at])
+        M[at] = new_master
+        F[at] = new_first
+        Q[at] = new_second
+        W[(z, y) + at] = new_master.astype(jnp.bfloat16)
+
+    every = slice(None)
 
     def source(b):
         return (z + Z - b // W_PIECES) % Z
@@ -326,17 +393,19 @@
 
     @pl.loop(0, W_PIECES)
     def _(b):
+        update(c, x, w_cols(b))
         own_a(b, y).start()
-
-    @pl.loop(0, G - W_PIECES)
+        gather_z(b).start()
+
+    @pl.loop(W_PIECES, G - W_PIECES)
     def _(j):
         gather_z(j).start()
 
     got_x.wait_recv()
     v_xc.start()
-    update(c, 1 - x)
+    update(c, 1 - x, every)
     got_c.wait_recv()
-    update(1 - c, x)
+    update(1 - c, x, every)
 
     @pl.loop(0, W_PIECES)
     def _(b):
@@ -363,7 +432,7 @@
         @pl.when(step == W_PIECES)
         def _():
             got_xc.wait_recv()
-            update(1 - c, 1 - x)
+            update(1 - c, 1 - x, every)
 
             @pl.loop(0, W_PIECES)
             def _(b):
@@ -389,9 +458,15 @@
     v_c.wait_send()
     v_xc.wait_send()
 
+    for copy in (to_core, chip_x, chip_y, far_x, far_y):
+        copy.wait_send()
+
+    @pl.loop(0, Z - 1)
+    def _(k):
+        plane(k, z).wait_send()
+
     @pl.loop(1, n)
     def _(k):
-        to_peer(B, m_sem, k).wait_send()
         to_peer(N, n_sem, k).wait_send()
 
     @pl.loop(0, C)
@@ -405,6 +480,10 @@
     @pl.loop(0, C - PIECES)
     def _(k):
         along_z(k).wait_send()
+
+    @pl.loop(0, G - W_PIECES)
+    def _(j):
+        gather_z(j).wait_send()
 
     @pl.loop(0, W_PIECES)
     def _(b):
@@ -419,10 +498,6 @@
         ha(b, x).wait_send()
         hb(b, y).wait_send()
         gc(b, c).wait_send()
-
-    @pl.loop(0, G - W_PIECES)
-    def _(j):
-        gather_z(j).wait_send()
 
 
 def write_out(*refs):
@@ -457,18 +532,18 @@
             pltpu.VMEM((Z, 2, t, cols), bf16),
             pltpu.VMEM((Z, 2, t, cols), bf16),
             pltpu.VMEM((Z, 2, t, cols), bf16),
-            pltpu.VMEM((Z - 1, 2, t, cols), bf16),
-            pltpu.VMEM((Z, 2, t, cols), bf16),
-            pltpu.VMEM((Z, 2, t, cols), bf16),
-            pltpu.VMEM((Z, 2, t, cols), bf16),
-            pltpu.VMEM((Z - 1, 2, t, cols), bf16),
+            pltpu.VMEM((Z, 2, t, cols), bf16),
+            pltpu.VMEM((Z, 2, t, cols), bf16),
+            pltpu.VMEM((Z, 2, t, cols), bf16),
+            pltpu.VMEM((Z, 2, t, cols), bf16),
+            pltpu.VMEM((Z, 2, t, cols), bf16),
             pltpu.VMEM(part, F32),
             pltpu.VMEM((Z, 2, 2, 2, 1, 128), F32),
-            pltpu.VMEM((Z, 2, 2, 2, 1, 128), F32),
+            pltpu.VMEM((PLANES + Z, 1, 128), F32),
             dma((PIECES * Z,)), dma((3,)),
             dma((2, PIECES * Z)), dma((2, PIECES * Z)), dma((2, PIECES * Z)),
             dma((2, PIECES * Z)), dma((2, PIECES * Z)), dma((2, PIECES * Z)),
-            dma((2, n)), dma((2, n)), dma((2, 3)),
+            dma((2, n)), dma((2, PLANES)), dma((2, Z)), pltpu.SemaphoreType.REGULAR((2,)), dma((2, 3)),
             dma((2, W_PIECES * Z)), dma((2, W_PIECES * Z)), dma((2, W_PIECES * Z)),
             dma((2, W_PIECES * Z)), dma((2, W_PIECES * Z)), dma((2, W_PIECES * Z)),
         ],

time: 68.7 us -> 65.4 us (0.952)
  Pallas kernels: 67.9 us -> 64.6 us
    pallas_call x1, Pallas kernels: 64.9 us -> 61.6 us  [body(): pl.pallas_call(functools.partial(kernel, Z, R, rows * cols), out_shape=[p...]
where the time goes in v3:
time: 65.4 us; the launch traced here: 65.2 us
  Pallas kernels  64.6 us (99%)
    pallas_call x1, Pallas kernels, body(): pl.pallas_call(functools.partial(kernel, Z, R, rows * cols), out_shape=[p...  61.6 us
    pallas_call x1, Pallas kernels, body(): pl.pallas_call(write_out, out_shape=[jax.ShapeDtypeStruct(*shape) for sha...  3.02 us

profile of v3, /device:TPU:1, one launch (start us, length us, event | category | flops | bytes accessed | tf_op | source)
XLA Modules:
  0.0 65.2 jit_solution(12657265310894528357)
XLA Ops:
  0.6 61.6 %shard_map.75 = (bf16[4,2,2,2,2,64,512]{6,5,4,3,2,1,0:T(8,128)(2,1)S(1)}, f32[2,2,2,64,512]{4,3,2,1,0:T(8,128)S(1)}, f32[2,2,2,64,512]{4,3,2,1,0:T(8,128)S(1)}, f32[2,2,2,64,512]{4,3,2,1,0:T(8,128)S(1)}) custom-call(bf16[4,2,2,2,2,64,512]{6,5,4,3,2,1,0:T(8,128)(2,1)} %bitcast.8, f32[2,2,2,64,512]{4,3,2,1,0:T(8,128)} %bitcast.9, ...), custom_call_target="tpu_custom_call" | custom-call | tf_op jit(solution)/shard_map/pallas_call | solution.py:523
  62.2 3.0 %shard_map.76 = (bf16[4,2,2,2,2,64,512]{6,5,4,3,2,1,0:T(8,128)(2,1)}, f32[2,2,2,64,512]{4,3,2,1,0:T(8,128)}, f32[2,2,2,64,512]{4,3,2,1,0:T(8,128)}, f32[2,2,2,64,512]{4,3,2,1,0:T(8,128)}) custom-call(bf16[4,2,2,2,2,64,512]{6,5,4,3,2,1,0:T(8,128)(2,1)S(1)} %get-tuple-element.12.refs_0_, f32[2,2,2,64,512]{4,3,2,1,0:T(8,128)S(1)} %get-tuple-element.13.refs_1_, ...), custom_call_target="tpu_custom_call" | custom-call | tf_op jit(solution)/shard_map/pallas_call | solution.py:557

commit v4 on v3

--- a/solution.py
+++ b/solution.py
@@ -12,7 +12,7 @@
 MESH = pl.DeviceIdType.MESH
 F32 = jnp.float32
 PIECES, TRAIL = 2, (2, 4)
-W_PIECES, W_TRAIL = 2, (2, 3)
+W_PIECES, W_TRAIL = 2, (2, 4)
 VMEM_BYTES = 63 * 1024 * 1024
 TOP = 2.0**14
 OWN, CORE, CHIP, FROM_X, FROM_Y, ALONG_X, ALONG_Y, FAR_X, FAR_Y, PLANES = range(10)
@@ -60,7 +60,9 @@
     d, r = lax.axis_index("dp"), lax.axis_index("rep")
     z, y = d // 2, d % 2
     x, c = r // 2, r % 2
-    C, G = PIECES * Z, W_PIECES * Z
+    t = g.shape[-2]
+    pieces, w_pieces = (count if t % (8 * count) == 0 else 1 for count in (PIECES, W_PIECES))
+    C, G = pieces * Z, w_pieces * Z
     to_x = (d, (1 - x) * 2 + c)
     to_y = (z * 2 + 1 - y, r)
     to_c = (d, x * 2 + 1 - c)
@@ -91,13 +93,11 @@
     def dest(k):
         return (z + 1 + k) % Z
 
-    def cols(q):
-        width = g.shape[-1] // PIECES
-        return pl.ds(pl.multiple_of((q % PIECES) * width, width), width)
-
-    def w_cols(q):
-        width = g.shape[-1] // W_PIECES
-        return pl.ds(pl.multiple_of((q % W_PIECES) * width, width), width)
+    def rows(q):
+        return pl.ds(pl.multiple_of((q % pieces) * (t // pieces), t // pieces), t // pieces)
+
+    def w_rows(q):
+        return pl.ds(pl.multiple_of((q % w_pieces) * (t // w_pieces), t // w_pieces), t // w_pieces)
 
     B[...] = jnp.zeros(B.shape, F32)
     barrier = pltpu.get_barrier_semaphore()
@@ -115,7 +115,7 @@
 
     def load(k):
         return pltpu.make_async_copy(
-            g.at[dest(k // PIECES), :, :, :, :, :, cols(k)], L.at[k // PIECES, :, :, :, :, :, cols(k)], load_sem.at[k]
+            g.at[dest(k // pieces), :, :, :, :, rows(k)], L.at[k // pieces, :, :, :, :, rows(k)], load_sem.at[k]
         )
 
     @pl.loop(0, C)
@@ -132,7 +132,7 @@
     @pl.loop(0, C)
     def _(k):
         load(k).wait()
-        size = jnp.abs(L[k // PIECES, :, :, :, :, :, cols(k)].astype(F32))
+        size = jnp.abs(L[k // pieces, :, :, :, :, rows(k)].astype(F32))
         lanes = jnp.max(size.reshape(-1, size.shape[-1]), axis=0, keepdims=True)
         best = B[OWN]
         for i in range(0, size.shape[-1], 128):
@@ -178,7 +178,7 @@
 
     def swap(k):
         return push(
-            L.at[k // PIECES, :, 1 - c, :, :, :, cols(k)], swapped.at[k // PIECES, :, :, :, :, cols(k)],
+            L.at[k // pieces, :, 1 - c, :, :, rows(k)], swapped.at[k // pieces, :, :, :, rows(k)],
             g_sem, (k,), to_c,
         )
 
@@ -190,24 +190,24 @@
         return jnp.maximum(jnp.max(B[index]), 1e-30)
 
     def first_a(k):
-        i, p = k // PIECES, cols(k)
-        return push(EA.at[i, :, :, p], RA.at[i, :, :, p], a1_sem, (k,), to_x)
+        i, p = k // pieces, rows(k)
+        return push(EA.at[i, :, p], RA.at[i, :, p], a1_sem, (k,), to_x)
 
     def first_b(k):
-        i, p = k // PIECES, cols(k)
-        return push(EB.at[i, :, :, p], RB.at[i, :, :, p], b1_sem, (k,), to_y)
+        i, p = k // pieces, rows(k)
+        return push(EB.at[i, :, p], RB.at[i, :, p], b1_sem, (k,), to_y)
 
     def second_a(k):
-        i, p = k // PIECES, cols(k)
-        return push(E2.at[i, 0, :, p], R2.at[i, 0, :, p], a2_sem, (k,), to_y)
+        i, p = k // pieces, rows(k)
+        return push(E2.at[i, 0, p], R2.at[i, 0, p], a2_sem, (k,), to_y)
 
     def second_b(k):
-        i, p = k // PIECES, cols(k)
-        return push(E2.at[i, 1, :, p], R2.at[i, 1, :, p], b2_sem, (k,), to_x)
+        i, p = k // pieces, rows(k)
+        return push(E2.at[i, 1, p], R2.at[i, 1, p], b2_sem, (k,), to_x)
 
     def along_z(k):
-        i, p = k // PIECES, cols(k)
-        return push(E3.at[i, :, :, p], R3.at[i, :, :, p], z_sem, (k,), to_z(dest(i)))
+        i, p = k // pieces, rows(k)
+        return push(E3.at[i, :, p], R3.at[i, :, p], z_sem, (k,), to_z(dest(i)))
 
     to_core.wait_recv()
     B[CHIP] = B[OWN] + B[CORE]
@@ -216,21 +216,21 @@
     own_scale = TOP / bound(CHIP)
 
     def stage1(k):
-        i, p = k // PIECES, cols(k)
+        i, p = k // pieces, rows(k)
         swap(k).wait_recv()
 
         def pair(yy, xx, h):
-            return L[i, yy, c, xx, h, :, p].astype(F32) + swapped[i, yy, xx, h, :, p].astype(F32)
+            return L[i, yy, c, xx, h, p].astype(F32) + swapped[i, yy, xx, h, p].astype(F32)
 
         for yy in range(2):
-            EA[i, yy, :, p] = encode(pair(yy, 1 - x, 0), own_scale)
+            EA[i, yy, p] = encode(pair(yy, 1 - x, 0), own_scale)
         first_a(k).start()
         for xx in range(2):
-            EB[i, xx, :, p] = encode(pair(1 - y, xx, 1), own_scale)
+            EB[i, xx, p] = encode(pair(1 - y, xx, 1), own_scale)
         first_b(k).start()
         for j in range(2):
-            S[i, j, x, 0, :, p] = pair(j, x, 0)
-            S[i, y, j, 1, :, p] = pair(y, j, 1)
+            S[i, j, x, 0, p] = pair(j, x, 0)
+            S[i, y, j, 1, p] = pair(y, j, 1)
 
     @pl.loop(0, TRAIL[0])
     def _(step):
@@ -247,15 +247,15 @@
     chain(1)
 
     def stage2(k):
-        i, p = k // PIECES, cols(k)
+        i, p = k // pieces, rows(k)
         first_a(k).wait_recv()
-        E2[i, 0, :, p] = encode(S[i, 1 - y, x, 0, :, p] + decode(RA[i, 1 - y, :, p], x_back), x_scale)
+        E2[i, 0, p] = encode(S[i, 1 - y, x, 0, p] + decode(RA[i, 1 - y, p], x_back), x_scale)
         second_a(k).start()
         first_b(k).wait_recv()
-        E2[i, 1, :, p] = encode(S[i, y, 1 - x, 1, :, p] + decode(RB[i, 1 - x, :, p], y_back), y_scale)
+        E2[i, 1, p] = encode(S[i, y, 1 - x, 1, p] + decode(RB[i, 1 - x, p], y_back), y_scale)
         second_b(k).start()
-        S[i, y, x, 0, :, p] = S[i, y, x, 0, :, p] + decode(RA[i, y, :, p], x_back)
-        S[i, y, x, 1, :, p] = S[i, y, x, 1, :, p] + decode(RB[i, x, :, p], y_back)
+        S[i, y, x, 0, p] = S[i, y, x, 0, p] + decode(RA[i, y, p], x_back)
+        S[i, y, x, 1, p] = S[i, y, x, 1, p] + decode(RB[i, x, p], y_back)
 
     @pl.loop(TRAIL[0], TRAIL[1])
     def _(step):
@@ -287,22 +287,22 @@
             stage2(step - TRAIL[0])
 
         k = step - TRAIL[1]
-        i, p = k // PIECES, cols(k)
+        i, p = k // pieces, rows(k)
         second_a(k).wait_recv()
         second_b(k).wait_recv()
-        both_a = S[i, y, x, 0, :, p] + decode(R2[i, 0, :, p], far_x_back)
-        both_b = S[i, y, x, 1, :, p] + decode(R2[i, 1, :, p], far_y_back)
-
-        @pl.when(k < C - PIECES)
-        def _():
-            E3[i, 0, :, p] = encode(both_a, plane_scale)
-            E3[i, 1, :, p] = encode(both_b, plane_scale)
+        both_a = S[i, y, x, 0, p] + decode(R2[i, 0, p], far_x_back)
+        both_b = S[i, y, x, 1, p] + decode(R2[i, 1, p], far_y_back)
+
+        @pl.when(k < C - pieces)
+        def _():
+            E3[i, 0, p] = encode(both_a, plane_scale)
+            E3[i, 1, p] = encode(both_b, plane_scale)
             along_z(k).start()
 
-        @pl.when(k >= C - PIECES)
-        def _():
-            S[i, y, x, 0, :, p] = both_a
-            S[i, y, x, 1, :, p] = both_b
+        @pl.when(k >= C - pieces)
+        def _():
+            S[i, y, x, 0, p] = both_a
+            S[i, y, x, 1, p] = both_b
 
     @pl.loop(0, Z - 1)
     def _(i):
@@ -310,20 +310,24 @@
         plane(i, source).wait_recv()
         back = bound(PLANES + source) / TOP
 
-        @pl.loop(0, PIECES)
+        @pl.loop(0, pieces)
         def _(j):
-            p = cols(j)
-            along_z(i * PIECES + j).wait_recv()
-            S[Z - 1, y, x, :, :, p] = S[Z - 1, y, x, :, :, p] + decode(R3[i, :, :, p], back)
+            p = rows(j)
+            along_z(i * pieces + j).wait_recv()
+            S[Z - 1, y, x, :, p] = S[Z - 1, y, x, :, p] + decode(R3[i, :, p], back)
 
     total = S[Z - 1, y, x]
     V[c, x] = total
     lanes = jnp.sum((total * total).reshape(-1, total.shape[-1]), axis=0, keepdims=True)
     N[z, y, x, c] = sum(lanes[:, i : i + 128] for i in range(0, total.shape[-1], 128))
 
-    @pl.loop(1, n)
-    def _(k):
-        to_peer(N, n_sem, n - k).start()
+    if n <= 32:
+        for k in range(n - 1, 0, -1):
+            to_peer(N, n_sem, k).start()
+    else:
+        @pl.loop(1, n)
+        def _(k):
+            to_peer(N, n_sem, n - k).start()
 
     v_x = push(V.at[c, x], V.at[c, x], v_sem, (0,), to_x)
     v_c = push(V.at[c, x], V.at[c, x], v_sem, (1,), to_c)
@@ -344,7 +348,7 @@
     factor = clip_factor(jnp.sum(N[...]), entries)
 
     def update(cc, xx, p):
-        at = (cc, xx, slice(None), slice(None), p)
+        at = (cc, xx, slice(None), p)
         new_master, new_first, new_second = adam_update(factor * V[at], M[at], F[at], Q[at])
         M[at] = new_master
         F[at] = new_first
@@ -354,67 +358,74 @@
     every = slice(None)
 
     def source(b):
-        return (z + Z - b // W_PIECES) % Z
+        return (z + Z - b // w_pieces) % Z
 
     def gather_z(j):
-        block = W.at[z, y, c, x, :, :, w_cols(j)]
-        return push(block, block, gz_sem, (j,), to_z(dest(j // W_PIECES)))
+        block = W.at[z, y, c, x, :, w_rows(j)]
+        return push(block, block, gz_sem, (j,), to_z(dest(j // w_pieces)))
 
     def got_z(j):
-        block = W.at[source(j + W_PIECES), y, c, x, :, :, w_cols(j)]
-        return push(block, block, gz_sem, (j,), to_z(dest(j // W_PIECES)))
+        block = W.at[source(j + w_pieces), y, c, x, :, w_rows(j)]
+        return push(block, block, gz_sem, (j,), to_z(dest(j // w_pieces)))
 
     def same(ref, sems, b, device):
         return push(ref, ref, sems, (b,), device)
 
     def own_a(b, yy):
-        return same(W.at[z, yy, c, x, :, :, w_cols(b)], ga_sem, b, to_y)
-
-    def own_h(b, xx):
-        return same(W.at[z, 1 - y, c, xx, :, :, w_cols(b)], ha_sem, b, to_x)
+        return same(W.at[z, yy, c, x, :, w_rows(b)], ga_sem, b, to_y)
+
+    def own_b(b, yy):
+        return same(W.at[z, yy, c, 1 - x, :, w_rows(b)], hb_sem, b, to_y)
 
     def own_c(b, cc):
-        return same(W.at[z, 1 - y, cc, :, :, :, w_cols(b)], gc_sem, b, to_c)
+        return same(W.at[z, 1 - y, cc, :, :, w_rows(b)], gc_sem, b, to_c)
 
     def ga(b, yy):
-        return same(W.at[source(b), yy, c, x, 0, :, w_cols(b)], ga_sem, b, to_y)
+        return same(W.at[source(b), yy, c, x, 0, w_rows(b)], ga_sem, b, to_y)
 
     def gb(b, xx):
-        return same(W.at[source(b), y, c, xx, 1, :, w_cols(b)], gb_sem, b, to_x)
+        return same(W.at[source(b), y, c, xx, 1, w_rows(b)], gb_sem, b, to_x)
 
     def ha(b, xx):
-        return same(W.at[source(b), :, c, xx, 0, :, w_cols(b)], ha_sem, b, to_x)
+        return same(W.at[source(b), :, c, xx, 0, w_rows(b)], ha_sem, b, to_x)
 
     def hb(b, yy):
-        return same(W.at[source(b), yy, c, :, 1, :, w_cols(b)], hb_sem, b, to_y)
+        return same(W.at[source(b), yy, c, :, 1, w_rows(b)], hb_sem, b, to_y)
 
     def gc(b, cc):
-        return same(W.at[source(b), :, cc, :, :, :, w_cols(b)], gc_sem, b, to_c)
-
-    @pl.loop(0, W_PIECES)
+        return same(W.at[source(b), :, cc, :, :, w_rows(b)], gc_sem, b, to_c)
+
+    @pl.loop(0, w_pieces)
     def _(b):
-        update(c, x, w_cols(b))
+        update(c, x, w_rows(b))
         own_a(b, y).start()
         gather_z(b).start()
 
-    @pl.loop(W_PIECES, G - W_PIECES)
+    @pl.loop(w_pieces, G - w_pieces)
     def _(j):
         gather_z(j).start()
 
     got_x.wait_recv()
     v_xc.start()
     update(c, 1 - x, every)
+
+    @pl.loop(0, w_pieces)
+    def _(b):
+        own_b(b, y).start()
+
     got_c.wait_recv()
     update(1 - c, x, every)
 
-    @pl.loop(0, W_PIECES)
-    def _(b):
-        own_a(b, 1 - y).wait_recv()
-        own_h(b, x).start()
-
-    @pl.loop(W_PIECES, G + W_TRAIL[1])
+    @pl.loop(w_pieces, G + W_TRAIL[1])
     def _(step):
-        @pl.when((step >= W_PIECES + W_TRAIL[0]) & (step < G + W_TRAIL[0]))
+        @pl.when(step < G)
+        def _():
+            b = step
+            got_z(b - w_pieces).wait_recv()
+            ga(b, y).start()
+            gb(b, x).start()
+
+        @pl.when((step >= w_pieces + W_TRAIL[0]) & (step < G + W_TRAIL[0]))
         def _():
             b = step - W_TRAIL[0]
             ga(b, 1 - y).wait_recv()
@@ -422,35 +433,29 @@
             gb(b, 1 - x).wait_recv()
             hb(b, y).start()
 
-        @pl.when(step < G)
-        def _():
-            b = step
-            got_z(b - W_PIECES).wait_recv()
-            ga(b, y).start()
-            gb(b, x).start()
-
-        @pl.when(step == W_PIECES)
+        @pl.when(step == w_pieces + 1)
         def _():
             got_xc.wait_recv()
             update(1 - c, 1 - x, every)
 
-            @pl.loop(0, W_PIECES)
+            @pl.loop(0, w_pieces)
             def _(b):
-                own_h(b, 1 - x).wait_recv()
+                own_a(b, 1 - y).wait_recv()
+                own_b(b, 1 - y).wait_recv()
                 own_c(b, c).start()
 
-        @pl.when(step >= W_PIECES + W_TRAIL[1])
+        @pl.when(step >= w_pieces + W_TRAIL[1])
         def _():
             b = step - W_TRAIL[1]
             ha(b, 1 - x).wait_recv()
             hb(b, 1 - y).wait_recv()
             gc(b, c).start()
 
-    @pl.loop(0, W_PIECES)
+    @pl.loop(0, w_pieces)
     def _(b):
         own_c(b, 1 - c).wait_recv()
 
-    @pl.loop(W_PIECES, G)
+    @pl.loop(w_pieces, G)
     def _(b):
         gc(b, 1 - c).wait_recv()
 
@@ -477,21 +482,21 @@
         second_a(k).wait_send()
         second_b(k).wait_send()
 
-    @pl.loop(0, C - PIECES)
+    @pl.loop(0, C - pieces)
     def _(k):
         along_z(k).wait_send()
 
-    @pl.loop(0, G - W_PIECES)
+    @pl.loop(0, G - w_pieces)
     def _(j):
         gather_z(j).wait_send()
 
-    @pl.loop(0, W_PIECES)
+    @pl.loop(0, w_pieces)
     def _(b):
         own_a(b, y).wait_send()
-        own_h(b, x).wait_send()
+        own_b(b, y).wait_send()
         own_c(b, c).wait_send()
 
-    @pl.loop(W_PIECES, G)
+    @pl.loop(w_pieces, G)
     def _(b):
         ga(b, y).wait_send()
         gb(b, x).wait_send()

time: 65.4 us -> 64.2 us (0.982)
  Pallas kernels: 64.6 us -> 63.3 us
    pallas_call x1, Pallas kernels: 61.6 us -> 60.2 us  [body(): pl.pallas_call(functools.partial(kernel, Z, R, rows * cols), out_shape=[p...]
where the time goes in v4:
time: 64.2 us; the launch traced here: 63.9 us
  Pallas kernels  63.3 us (99%)
    pallas_call x1, Pallas kernels, body(): pl.pallas_call(functools.partial(kernel, Z, R, rows * cols), out_shape=[p...  60.2 us
    pallas_call x1, Pallas kernels, body(): pl.pallas_call(write_out, out_shape=[jax.ShapeDtypeStruct(*shape) for sha...  3.02 us

profile of v4, /device:TPU:1, one launch (start us, length us, event | category | flops | bytes accessed | tf_op | source)
XLA Modules:
  0.0 63.9 jit_solution(17907431265635821275)
XLA Ops:
  0.6 60.2 %shard_map.75 = (bf16[4,2,2,2,2,64,512]{6,5,4,3,2,1,0:T(8,128)(2,1)S(1)}, f32[2,2,2,64,512]{4,3,2,1,0:T(8,128)S(1)}, f32[2,2,2,64,512]{4,3,2,1,0:T(8,128)S(1)}, f32[2,2,2,64,512]{4,3,2,1,0:T(8,128)S(1)}) custom-call(bf16[4,2,2,2,2,64,512]{6,5,4,3,2,1,0:T(8,128)(2,1)} %bitcast.8, f32[2,2,2,64,512]{4,3,2,1,0:T(8,128)} %bitcast.9, ...), custom_call_target="tpu_custom_call" | custom-call | tf_op jit(solution)/shard_map/pallas_call | solution.py:528
  60.9 3.0 %shard_map.76 = (bf16[4,2,2,2,2,64,512]{6,5,4,3,2,1,0:T(8,128)(2,1)}, f32[2,2,2,64,512]{4,3,2,1,0:T(8,128)}, f32[2,2,2,64,512]{4,3,2,1,0:T(8,128)}, f32[2,2,2,64,512]{4,3,2,1,0:T(8,128)}) custom-call(bf16[4,2,2,2,2,64,512]{6,5,4,3,2,1,0:T(8,128)(2,1)S(1)} %get-tuple-element.12.refs_0_, f32[2,2,2,64,512]{4,3,2,1,0:T(8,128)S(1)} %get-tuple-element.13.refs_1_, ...), custom_call_target="tpu_custom_call" | custom-call | tf_op jit(solution)/shard_map/pallas_call | solution.py:562

commit v5 on v4

--- a/solution.py
+++ b/solution.py
@@ -13,6 +13,7 @@
 F32 = jnp.float32
 PIECES, TRAIL = 2, (2, 4)
 W_PIECES, W_TRAIL = 2, (2, 4)
+SUM_ORDER, GATHER_ORDER = (1, 2, 0), (2, 0, 1)
 VMEM_BYTES = 63 * 1024 * 1024
 TOP = 2.0**14
 OWN, CORE, CHIP, FROM_X, FROM_Y, ALONG_X, ALONG_Y, FAR_X, FAR_Y, PLANES = range(10)
@@ -90,8 +91,19 @@
 
     below, above = z, Z - 1 - z
 
+    def mate(i, order):
+        flips = (jnp.where(z % 2 == 0, z + 1, z - 1), (z + 2) % Z, Z - 1 - z)
+        first, second, third = (flips[m] for m in order)
+        return jnp.where(i == 0, first, jnp.where(i == 1, second, third))
+
+    def goes_to(i, order):
+        return mate(i, order) if Z == 4 else (z + 1 + i) % Z
+
+    def comes_from(i, order):
+        return mate(i, order) if Z == 4 else (z + Z - 1 - i) % Z
+
     def dest(k):
-        return (z + 1 + k) % Z
+        return jnp.where(k == Z - 1, z, goes_to(k, SUM_ORDER))
 
     def rows(q):
         return pl.ds(pl.multiple_of((q % pieces) * (t // pieces), t // pieces), t // pieces)
@@ -306,7 +318,7 @@
 
     @pl.loop(0, Z - 1)
     def _(i):
-        source = (z + Z - 1 - i) % Z
+        source = comes_from(i, SUM_ORDER)
         plane(i, source).wait_recv()
         back = bound(PLANES + source) / TOP
 
@@ -358,15 +370,15 @@
     every = slice(None)
 
     def source(b):
-        return (z + Z - b // w_pieces) % Z
+        return jnp.where(b < w_pieces, z, comes_from(b // w_pieces - 1, GATHER_ORDER))
 
     def gather_z(j):
         block = W.at[z, y, c, x, :, w_rows(j)]
-        return push(block, block, gz_sem, (j,), to_z(dest(j // w_pieces)))
+        return push(block, block, gz_sem, (j,), to_z(goes_to(j // w_pieces, GATHER_ORDER)))
 
     def got_z(j):
         block = W.at[source(j + w_pieces), y, c, x, :, w_rows(j)]
-        return push(block, block, gz_sem, (j,), to_z(dest(j // w_pieces)))
+        return push(block, block, gz_sem, (j,), to_z(goes_to(j // w_pieces, GATHER_ORDER)))
 
     def same(ref, sems, b, device):
         return push(ref, ref, sems, (b,), device)

time: 64.2 us -> 62.2 us (0.969)
  Pallas kernels: 63.3 us -> 61.4 us
    pallas_call x1, Pallas kernels: 60.2 us -> 58.4 us  [body(): pl.pallas_call(functools.partial(kernel, Z, R, rows * cols), out_shape=[p...]
where the time goes in v5:
time: 62.2 us; the launch traced here: 62 us
  Pallas kernels  61.4 us (99%)
  between operations  0.64 us (1%)
    pallas_call x1, Pallas kernels, body(): pl.pallas_call(functools.partial(kernel, Z, R, rows * cols), out_shape=[p...  58.4 us
    pallas_call x1, Pallas kernels, body(): pl.pallas_call(write_out, out_shape=[jax.ShapeDtypeStruct(*shape) for sha...  3.02 us

profile of v5, /device:TPU:1, one launch (start us, length us, event | category | flops | bytes accessed | tf_op | source)
XLA Modules:
  0.0 62.0 jit_solution(10792350186539904314)
XLA Ops:
  0.6 58.4 %shard_map.75 = (bf16[4,2,2,2,2,64,512]{6,5,4,3,2,1,0:T(8,128)(2,1)S(1)}, f32[2,2,2,64,512]{4,3,2,1,0:T(8,128)S(1)}, f32[2,2,2,64,512]{4,3,2,1,0:T(8,128)S(1)}, f32[2,2,2,64,512]{4,3,2,1,0:T(8,128)S(1)}) custom-call(bf16[4,2,2,2,2,64,512]{6,5,4,3,2,1,0:T(8,128)(2,1)} %bitcast.8, f32[2,2,2,64,512]{4,3,2,1,0:T(8,128)} %bitcast.9, ...), custom_call_target="tpu_custom_call" | custom-call | tf_op jit(solution)/shard_map/pallas_call | solution.py:540
  59.0 3.0 %shard_map.76 = (bf16[4,2,2,2,2,64,512]{6,5,4,3,2,1,0:T(8,128)(2,1)}, f32[2,2,2,64,512]{4,3,2,1,0:T(8,128)}, f32[2,2,2,64,512]{4,3,2,1,0:T(8,128)}, f32[2,2,2,64,512]{4,3,2,1,0:T(8,128)}) custom-call(bf16[4,2,2,2,2,64,512]{6,5,4,3,2,1,0:T(8,128)(2,1)S(1)} %get-tuple-element.12.refs_0_, f32[2,2,2,64,512]{4,3,2,1,0:T(8,128)S(1)} %get-tuple-element.13.refs_1_, ...), custom_call_target="tpu_custom_call" | custom-call | tf_op jit(solution)/shard_map/pallas_call | solution.py:574

commit v6 on v5

--- a/solution.py
+++ b/solution.py
@@ -445,7 +445,7 @@
             gb(b, 1 - x).wait_recv()
             hb(b, y).start()
 
-        @pl.when(step == w_pieces + 1)
+        @pl.when(step == w_pieces + 3)
         def _():
             got_xc.wait_recv()
             update(1 - c, 1 - x, every)

time: 62.2 us -> 62 us (level)
  no operation moved by 1% of the time
where the time goes in v6:
time: 62 us; the launch traced here: 61.8 us
  Pallas kernels  61.2 us (99%)
  between operations  0.64 us (1%)
    pallas_call x1, Pallas kernels, body(): pl.pallas_call(functools.partial(kernel, Z, R, rows * cols), out_shape=[p...  58.2 us
    pallas_call x1, Pallas kernels, body(): pl.pallas_call(write_out, out_shape=[jax.ShapeDtypeStruct(*shape) for sha...  3.02 us

profile of v6, /device:TPU:1, one launch (start us, length us, event | category | flops | bytes accessed | tf_op | source)
XLA Modules:
  0.0 61.8 jit_solution(5995826260599921792)
XLA Ops:
  0.6 58.2 %shard_map.75 = (bf16[4,2,2,2,2,64,512]{6,5,4,3,2,1,0:T(8,128)(2,1)S(1)}, f32[2,2,2,64,512]{4,3,2,1,0:T(8,128)S(1)}, f32[2,2,2,64,512]{4,3,2,1,0:T(8,128)S(1)}, f32[2,2,2,64,512]{4,3,2,1,0:T(8,128)S(1)}) custom-call(bf16[4,2,2,2,2,64,512]{6,5,4,3,2,1,0:T(8,128)(2,1)} %bitcast.8, f32[2,2,2,64,512]{4,3,2,1,0:T(8,128)} %bitcast.9, ...), custom_call_target="tpu_custom_call" | custom-call | tf_op jit(solution)/shard_map/pallas_call | solution.py:540
  58.8 3.0 %shard_map.76 = (bf16[4,2,2,2,2,64,512]{6,5,4,3,2,1,0:T(8,128)(2,1)}, f32[2,2,2,64,512]{4,3,2,1,0:T(8,128)}, f32[2,2,2,64,512]{4,3,2,1,0:T(8,128)}, f32[2,2,2,64,512]{4,3,2,1,0:T(8,128)}) custom-call(bf16[4,2,2,2,2,64,512]{6,5,4,3,2,1,0:T(8,128)(2,1)S(1)} %get-tuple-element.12.refs_0_, f32[2,2,2,64,512]{4,3,2,1,0:T(8,128)S(1)} %get-tuple-element.13.refs_1_, ...), custom_call_target="tpu_custom_call" | custom-call | tf_op jit(solution)/shard_map/pallas_call | solution.py:574

commit v7 on v6

--- a/solution.py
+++ b/solution.py
@@ -425,9 +425,6 @@
     def _(b):
         own_b(b, y).start()
 
-    got_c.wait_recv()
-    update(1 - c, x, every)
-
     @pl.loop(w_pieces, G + W_TRAIL[1])
     def _(step):
         @pl.when(step < G)
@@ -447,6 +444,8 @@
 
         @pl.when(step == w_pieces + 3)
         def _():
+            got_c.wait_recv()
+            update(1 - c, x, every)
             got_xc.wait_recv()
             update(1 - c, 1 - x, every)
 

time: 62 us -> 62 us (level)
  no operation moved by 1% of the time
where the time goes in v7:
time: 62 us; the launch traced here: 61.8 us
  Pallas kernels  61.2 us (99%)
  between operations  0.64 us (1%)
    pallas_call x1, Pallas kernels, body(): pl.pallas_call(functools.partial(kernel, Z, R, rows * cols), out_shape=[p...  58.2 us
    pallas_call x1, Pallas kernels, body(): pl.pallas_call(write_out, out_shape=[jax.ShapeDtypeStruct(*shape) for sha...  3.02 us

profile of v7, /device:TPU:1, one launch (start us, length us, event | category | flops | bytes accessed | tf_op | source)
XLA Modules:
  0.0 61.8 jit_solution(10809169677075825436)
XLA Ops:
  0.6 58.2 %shard_map.75 = (bf16[4,2,2,2,2,64,512]{6,5,4,3,2,1,0:T(8,128)(2,1)S(1)}, f32[2,2,2,64,512]{4,3,2,1,0:T(8,128)S(1)}, f32[2,2,2,64,512]{4,3,2,1,0:T(8,128)S(1)}, f32[2,2,2,64,512]{4,3,2,1,0:T(8,128)S(1)}) custom-call(bf16[4,2,2,2,2,64,512]{6,5,4,3,2,1,0:T(8,128)(2,1)} %bitcast.8, f32[2,2,2,64,512]{4,3,2,1,0:T(8,128)} %bitcast.9, ...), custom_call_target="tpu_custom_call" | custom-call | tf_op jit(solution)/shard_map/pallas_call | solution.py:539
  58.8 3.0 %shard_map.76 = (bf16[4,2,2,2,2,64,512]{6,5,4,3,2,1,0:T(8,128)(2,1)}, f32[2,2,2,64,512]{4,3,2,1,0:T(8,128)}, f32[2,2,2,64,512]{4,3,2,1,0:T(8,128)}, f32[2,2,2,64,512]{4,3,2,1,0:T(8,128)}) custom-call(bf16[4,2,2,2,2,64,512]{6,5,4,3,2,1,0:T(8,128)(2,1)S(1)} %get-tuple-element.12.refs_0_, f32[2,2,2,64,512]{4,3,2,1,0:T(8,128)S(1)} %get-tuple-element.13.refs_1_, ...), custom_call_target="tpu_custom_call" | custom-call | tf_op jit(solution)/shard_map/pallas_call | solution.py:573
